TPU v7x, 32 devices: a whole 2x2x4 slice. The times are simulated.
32 devices in a mesh: grp: 4 (over x, core), mem: 8 (over z, y).
Axes of the slice: x: 2, y: 2, z: 4, core: 2. Of those that a mesh axis runs over, the one named last changes fastest.
Arguments:
- child_field: float32 [2, 1024, 4096], P(None, None, ('grp', 'mem')), may hold values from -6 to 6
- theta_interp: float32 [64, 32], replicated, may hold values from -1 to 1
- phi_interp: float32 [64, 32], replicated, may hold values from -1 to 1
- child_phase: float32 [8, 4096], replicated, may hold values from -3.140625 to 3.140625
- translation: float32 [2, 316, 4096], P(None, None, 'mem'), may hold values from -0.3125 to 0.3125
- inter_source: int32 [32, 24], P('grp'), may hold values from 0 to 31, as said below
- inter_kind: int32 [32, 24], P('grp'), may hold values from 0 to 315
- inter_count: int32 [32], P('grp'), may hold values from 6 to 24
Outputs:
- child_out: float32 [2, 1024, 4096], P(None, None, ('grp', 'mem'))
Inputs may be any that keep to these rules, and one draw needn't show every extreme that they name: The source box of every slot lies in its target's group of 8 consecutive parent boxes or in one of the two groups beside it: inter_source[t, k] // 8 differs from t // 8 by at most one. Slots from inter_count[t] on are unused.
All inputs are finite; a program needn't handle non-finite values.
Results may differ from a plain program's by a relative error of at most 0.0003.
Values sent between devices are 32-bit elements; how exact they have to be, the bound alone decides.
No kernel may reach another device: no remote copies, remote signals or barrier semaphores. Data moves between devices by JAX's collectives and lax.ppermute only.
A program may use at most 64 MiB of HBM per device.

v0:
```python
import functools

import jax
import jax.numpy as jnp
from jax import lax
from jax.experimental import pallas as pl
from jax.experimental.pallas import tpu as pltpu
from jax.sharding import PartitionSpec as P

f32 = jnp.float32
bf16 = jnp.bfloat16
SUB = 8
BLOCK = 256
UNROLL = 4


def split(x):
    hi = x.astype(bf16)
    lo = (x - hi.astype(f32)).astype(bf16)
    return hi, lo


def mm(a, b):
    return jnp.dot(a, b, preferred_element_type=f32)


def mm_tn(a, b):
    return lax.dot_general(a, b, (((0,), (0,)), ((), ())), preferred_element_type=f32)


def iota(shape, dim):
    return lax.broadcasted_iota(jnp.int32, shape, dim)


def picker(shape, test):
    return jnp.where(test(iota(shape, 0), iota(shape, 1)), 1.0, 0.0).astype(bf16)


def sincos(q):
    r = q * 0.5
    z = r * r
    s = 1.0 / 6227020800.0
    for c in (-1.0 / 39916800.0, 1.0 / 362880.0, -1.0 / 5040.0, 1.0 / 120.0, -1.0 / 6.0, 1.0):
        s = s * z + c
    s = s * r
    k = 1.0 / 479001600.0
    for c in (-1.0 / 3628800.0, 1.0 / 40320.0, -1.0 / 720.0, 1.0 / 24.0, -0.5, 1.0):
        k = k * z + c
    return 2.0 * s * k, 1.0 - 2.0 * s * s


def aggregate_kernel(x_ref, theta_ref, phi_ref, phase_ref, o_ref, mid_ref, cos_ref, sin_ref):
    coarse_t, fine_t = theta_ref.shape
    coarse_p, fine_p = phi_ref.shape
    groups = coarse_p // SUB
    span = BLOCK // fine_p
    per_member = o_ref.shape[3]
    waves = o_ref.shape[2]
    branch = phase_ref.shape[0]
    columns = branch * waves

    spread_t = picker((coarse_t, coarse_t * SUB), lambda r, c: r == c // SUB)
    big = (fine_t * SUB, coarse_t * SUB)
    keep = iota(big, 0) % SUB == iota(big, 1) % SUB

    def theta_block(part):
        rows = mm_tn(part, spread_t)
        rows = jnp.broadcast_to(rows[:, None, :], (fine_t, SUB, coarse_t * SUB)).reshape(big)
        return jnp.where(keep, rows, 0.0).astype(bf16)

    th, tl = split(theta_ref[...])
    kh, kl = theta_block(th), theta_block(tl)
    weights = jnp.concatenate([kh, kh, kl], axis=1)

    spread_p = picker((fine_p, BLOCK), lambda r, c: r == c % fine_p)
    small = (span * coarse_p, BLOCK)
    diag = iota(small, 0) // coarse_p == iota(small, 1) // fine_p

    def phi_block(part):
        rows = mm(part, spread_p)
        rows = jnp.concatenate([rows] * span, axis=0)
        return jnp.where(diag, rows, 0.0).astype(bf16)

    ph, pl_ = split(phi_ref[...])
    bh, bl = phi_block(ph), phi_block(pl_)
    phi_weights = jnp.concatenate([bh, bh, bl], axis=0)

    sine, cosine = sincos(phase_ref[...])
    cos_ref[...] = cosine
    sin_ref[...] = sine

    for g in range(groups):
        parts = [x_ref[c, :, g].reshape(coarse_t * SUB, columns) for c in range(2)]
        hi, lo = split(jnp.concatenate(parts, axis=1))
        middle = mm(weights, jnp.concatenate([hi, lo, hi], axis=0))
        mid_ref[:, g] = middle.reshape(fine_t, SUB, 2 * columns)

    unit = min(BLOCK, per_member)

    def body(step, carry):
        start = step * BLOCK
        rows = mid_ref[pl.ds(step * span, span)].reshape(span * coarse_p, 2 * columns)
        hi, lo = split(rows.T)
        fine = mm(jnp.concatenate([hi, lo, hi], axis=1), phi_weights)
        real = fine[:columns].reshape(branch, waves, BLOCK)
        imag = fine[columns:].reshape(branch, waves, BLOCK)
        lanes = pl.ds(pl.multiple_of(start, BLOCK), BLOCK)
        c = cos_ref[:, lanes][:, None, :]
        s = sin_ref[:, lanes][:, None, :]
        out_real = jnp.sum(real * c - imag * s, axis=0)
        out_imag = jnp.sum(imag * c + real * s, axis=0)
        for piece in range(BLOCK // unit):
            at = start + piece * unit
            member = at // per_member
            offset = pl.multiple_of(at - member * per_member, unit)
            here = slice(piece * unit, (piece + 1) * unit)
            o_ref[member, 0, :, pl.ds(offset, unit)] = out_real[:, here]
            o_ref[member, 1, :, pl.ds(offset, unit)] = out_imag[:, here]
        return carry

    lax.fori_loop(0, fine_t // span, body, 0)


def translate_kernel(source_ref, kind_ref, count_ref, base_ref, factor_ref, own_ref, before_ref, after_ref, o_ref, all_ref, sems):
    members = own_ref.shape[0]
    targets, slots = source_ref.shape
    copies = [
        pltpu.make_async_copy(ref, all_ref.at[pl.ds(i * members, members)], sems.at[i])
        for i, ref in enumerate((before_ref, own_ref, after_ref))
    ]
    for copy in copies:
        copy.start()
    for copy in copies:
        copy.wait()
    base = base_ref[0]
    waves, directions = o_ref.shape[2:]

    def target_body(t, carry):
        count = count_ref[t]

        def slot_body(step, acc):
            real, imag = acc
            for i in range(UNROLL):
                k = step * UNROLL + i
                live = k < count
                at = jnp.where(live, source_ref[t, k] - base, 0)
                kind = jnp.where(live, kind_ref[t, k], 0)
                weight = jnp.where(live, 1.0, 0.0).astype(f32)
                factor = factor_ref[kind] * weight
                fr = factor[0:1]
                fi = factor[1:2]
                sr = all_ref[at, 0]
                si = all_ref[at, 1]
                real = real + (fr * sr - fi * si)
                imag = imag + (fr * si + fi * sr)
            return real, imag

        zero = jnp.zeros((waves, directions), f32)
        real, imag = lax.fori_loop(0, (count + UNROLL - 1) // UNROLL, slot_body, (zero, zero))
        o_ref[t, 0] = real
        o_ref[t, 1] = imag
        return carry

    lax.fori_loop(0, targets, target_body, 0)


def disaggregate_kernel(r_ref, theta_ref, phi_ref, phase_ref, o_ref, mid_ref, cos_ref, sin_ref):
    coarse_t, fine_t = theta_ref.shape
    coarse_p, fine_p = phi_ref.shape
    groups = coarse_p // SUB
    span = BLOCK // fine_p
    per_member = r_ref.shape[3]
    waves = r_ref.shape[2]
    branch = phase_ref.shape[0]
    columns = branch * waves

    spread_t = picker((fine_t, fine_t * SUB), lambda r, c: r == c // SUB)
    big = (coarse_t * SUB, fine_t * SUB)
    keep = iota(big, 0) % SUB == iota(big, 1) % SUB

    def theta_block(part):
        rows = mm(part, spread_t)
        rows = jnp.broadcast_to(rows[:, None, :], (coarse_t, SUB, fine_t * SUB)).reshape(big)
        return jnp.where(keep, rows, 0.0).astype(bf16)

    th, tl = split(theta_ref[...])
    kh, kl = theta_block(th), theta_block(tl)
    weights = jnp.concatenate([kh, kh, kl], axis=1)

    narrow = span * coarse_p
    spread_p = picker((coarse_p, narrow), lambda r, c: r == c % coarse_p)
    small = (BLOCK, narrow)
    diag = iota(small, 0) // fine_p == iota(small, 1) // coarse_p

    def phi_block(part):
        rows = mm_tn(part, spread_p)
        rows = jnp.concatenate([rows] * span, axis=0)
        return jnp.where(diag, rows, 0.0).astype(bf16)

    ph, pl_ = split(phi_ref[...])
    phi_weights = jnp.concatenate([phi_block(ph), phi_block(pl_)], axis=1)

    sine, cosine = sincos(phase_ref[...])
    cos_ref[...] = cosine
    sin_ref[...] = sine
    unit = min(BLOCK, per_member)

    def body(step, carry):
        start = step * BLOCK
        pieces = []
        for piece in range(BLOCK // unit):
            at = start + piece * unit
            member = at // per_member
            offset = pl.multiple_of(at - member * per_member, unit)
            pieces.append([r_ref[member, c, :, pl.ds(offset, unit)] for c in range(2)])
        real = jnp.concatenate([p[0] for p in pieces], axis=1)[None]
        imag = jnp.concatenate([p[1] for p in pieces], axis=1)[None]
        lanes = pl.ds(pl.multiple_of(start, BLOCK), BLOCK)
        c = cos_ref[:, lanes][:, None, :]
        s = sin_ref[:, lanes][:, None, :]
        local = jnp.concatenate(
            [
                (real * c + imag * s).reshape(columns, BLOCK),
                (imag * c - real * s).reshape(columns, BLOCK),
            ],
            axis=0,
        )
        hi, lo = split(local)
        y = mm(jnp.concatenate([hi, lo], axis=0), phi_weights)
        rows = 2 * columns
        folded = y[:rows, :narrow] + (y[rows:, :narrow] + y[:rows, narrow:])
        mid_ref[pl.ds(step * span, span)] = folded.T.reshape(span, groups, SUB, rows)
        return carry

    lax.fori_loop(0, fine_t // span, body, 0)

    for g in range(groups):
        hi, lo = split(mid_ref[:, g].reshape(fine_t * SUB, 2 * columns))
        coarse = mm(weights, jnp.concatenate([hi, lo, hi], axis=0))
        o_ref[0, :, g] = coarse[:, :columns].reshape(coarse_t, SUB, columns)
        o_ref[1, :, g] = coarse[:, columns:].reshape(coarse_t, SUB, columns)


def vmem():
    return pl.BlockSpec(memory_space=pltpu.VMEM)


def smem():
    return pl.BlockSpec(memory_space=pltpu.SMEM)


def hbm():
    return pl.BlockSpec(memory_space=pltpu.HBM)


def per_device(
    child_field,
    theta_interp,
    phi_interp,
    child_phase,
    translation,
    inter_source,
    inter_kind,
    inter_count,
    *,
    interpret=False,
):
    call = functools.partial(pl.pallas_call, interpret=interpret)
    branch, fine = child_phase.shape
    columns = child_field.shape[2]
    waves = columns // branch
    fine_t, coarse_t = theta_interp.shape
    fine_p, coarse_p = phi_interp.shape
    groups = coarse_p // SUB
    members = lax.axis_size("mem")
    grp_count = lax.axis_size("grp")
    per_member = fine // members
    theta_t = theta_interp.T
    phi_t = phi_interp.T
    scratch = [
        pltpu.VMEM((fine_t, groups, SUB, 2 * columns), f32),
        pltpu.VMEM((branch, fine), f32),
        pltpu.VMEM((branch, fine), f32),
    ]
    block = jax.ShapeDtypeStruct((members, 2, waves, per_member), f32)
    summed = call(
        aggregate_kernel,
        out_shape=block,
        in_specs=[vmem()] * 4,
        out_specs=vmem(),
        scratch_shapes=scratch,
    )(child_field.reshape(2, coarse_t, groups, SUB, columns), theta_t, phi_t, child_phase)

    own = lax.all_to_all(summed, "mem", split_axis=0, concat_axis=0, tiled=True)
    up = [(i, i + 1) for i in range(grp_count - 1)]
    before = lax.ppermute(own, "grp", up)
    after = lax.ppermute(own, "grp", [(j, i) for i, j in up])
    base = ((lax.axis_index("grp") - 1) * members).astype(jnp.int32).reshape(1)

    incoming = call(
        translate_kernel,
        out_shape=block,
        in_specs=[smem()] * 4 + [vmem()] + [hbm()] * 3,
        out_specs=vmem(),
        scratch_shapes=[
            pltpu.VMEM((3 * members, 2, waves, per_member), f32),
            pltpu.SemaphoreType.DMA((3,)),
        ],
    )(inter_source, inter_kind, inter_count, base, jnp.transpose(translation, (1, 0, 2)), own, before, after)

    returned = lax.all_to_all(incoming, "mem", split_axis=0, concat_axis=0, tiled=True)
    out = call(
        disaggregate_kernel,
        out_shape=jax.ShapeDtypeStruct((2, coarse_t, groups, SUB, columns), f32),
        in_specs=[vmem()] * 4,
        out_specs=vmem(),
        scratch_shapes=scratch,
    )(returned, theta_t, phi_t, child_phase)
    return out.reshape(child_field.shape)


def solution(mesh):
    return jax.shard_map(
        per_device,
        mesh=mesh,
        in_specs=(
            P(None, None, ("grp", "mem")),
            P(),
            P(),
            P(),
            P(None, None, "mem"),
            P("grp", None),
            P("grp", None),
            P("grp"),
        ),
        out_specs=P(None, None, ("grp", "mem")),
        check_vma=False,
    )
```

profile of v0, /device:TPU:1, one launch (start us, length us, event | category | flops | bytes accessed | tf_op | source)
XLA Modules:
  0.0 69.8 jit_solution(171957901522382450)
XLA Ops:
  0.0 7.8 %shard_map.82 = f32[8,2,16,512]{3,2,1,0:T(8,128)} custom-call(f32[2,32,4,8,128]{4,3,2,1,0:T(8,128)} %bitcast.7, f32[32,64]{1,0:T(8,128)} %bitcast.8, f32[32,64]{1,0:T(8,128)} %bitcast.10, f32[8,4096]{1,0:T(8,128)} %phase_ref.3), custom_call_target="tpu_custom_call" | custom-call | tf_op jit(solution)/shard_map/pallas_call | solution.py:286
  7.8 20.1 %all_to_all.10.own_ref = f32[8,2,16,512]{3,2,1,0:T(8,128)S(1)} all-to-all(f32[8,2,16,512]{3,2,1,0:T(8,128)} %shard_map.82), channel_id=1, replica_groups=mesh['grp'=4,'mem'=8] {'mem'}, dimensions={0} | all-to-all | bytes 1048576 | tf_op jit(solution)/shard_map/all_to_all | solution.py:294
  27.9 0.0 copy-start
  27.9 3.7 %collective-permute-start.1 = (f32[8,2,16,512]{3,2,1,0:T(8,128)S(1)}, f32[8,2,16,512]{3,2,1,0:T(8,128)S(1)}, u32[]{:S(2)}, u32[]{:S(2)}) collective-permute-start(f32[8,2,16,512]{3,2,1,0:T(8,128)S(1)} %all_to_all.10.own_ref), channel_id=1, source_target_pairs={{8,0},{16,8},{24,16},{9,1},{17,9},{25,17},{10,2},{18,10},{26,18},{... | collective-permute-start | bytes 1572872 | tf_op jit(solution)/shard_map/ppermute | solution.py:297
  31.6 3.0 %collective-permute-start = (f32[8,2,16,512]{3,2,1,0:T(8,128)S(1)}, f32[8,2,16,512]{3,2,1,0:T(8,128)S(1)}, u32[]{:S(2)}, u32[]{:S(2)}) collective-permute-start(f32[8,2,16,512]{3,2,1,0:T(8,128)S(1)} %all_to_all.10.own_ref), channel_id=1, source_target_pairs={{0,8},{8,16},{16,24},{1,9},{9,17},{17,25},{2,10},{10,18},{18,26},{... | collective-permute-start | bytes 1572872 | tf_op jit(solution)/shard_map/ppermute | solution.py:296
  34.6 4.9 %collective-permute-done.1.after_ref = f32[8,2,16,512]{3,2,1,0:T(8,128)S(1)} collective-permute-done((f32[8,2,16,512]{3,2,1,0:T(8,128)S(1)}, f32[8,2,16,512]{3,2,1,0:T(8,128)S(1)}, u32[]{:S(2)}, u32[]{:S(2)}) %collective-permute-start.1) | collective-permute-done | bytes 524320 | tf_op jit(solution)/shard_map/ppermute | solution.py:297
  39.5 0.0 copy-start.1
  39.5 1.2 %collective-permute-done.before_ref = f32[8,2,16,512]{3,2,1,0:T(8,128)S(1)} collective-permute-done((f32[8,2,16,512]{3,2,1,0:T(8,128)S(1)}, f32[8,2,16,512]{3,2,1,0:T(8,128)S(1)}, u32[]{:S(2)}, u32[]{:S(2)}) %collective-permute-start) | collective-permute-done | bytes 524320 | tf_op jit(solution)/shard_map/ppermute | solution.py:296
  40.7 0.0 copy-start.2
  40.7 0.0 copy-done
  40.7 0.0 copy-done.1
  40.7 0.8 %copy-done.2 = f32[8,2,16,512]{3,2,1,0:T(8,128)} copy-done((f32[8,2,16,512]{3,2,1,0:T(8,128)}, f32[8,2,16,512]{3,2,1,0:T(8,128)S(1)}, u32[]{:S(2)}) %copy-start.2) | copy-done | bytes 524312
  41.5 5.4 %shard_map.83 = f32[8,2,16,512]{3,2,1,0:T(8,128)} custom-call(s32[8,24]{1,0:T(8,128)} %source_ref.1, s32[8,24]{1,0:T(8,128)} %kind_ref.1, s32[8]{0:T(128)} %count_ref.1, s32[1]{0:T(128)} %bitcast.base_ref, f32[316,2,512]{2,1,0:T(2,128)} %bitcast.6, f32[8,2,16,512]{3,2,1,0:T(8,128)} %copy-done, f32[8,2,16,512]{3,2,1,0:T(8,128)} %copy-done.2, ...), custom_call_target="tpu_custom_call" | custom-call | tf_op jit(solution)/shard_map/pallas_call | solution.py:300
  46.9 14.4 %all_to_all.11.r_ref = f32[8,2,16,512]{3,2,1,0:T(8,128)} all-to-all(f32[8,2,16,512]{3,2,1,0:T(8,128)} %shard_map.83), channel_id=1, replica_groups=mesh['grp'=4,'mem'=8] {'mem'}, dimensions={0} | all-to-all | bytes 1048576 | tf_op jit(solution)/shard_map/all_to_all | solution.py:311
  61.4 8.4 %shard_map.84 = f32[2,32,4,8,128]{4,3,2,1,0:T(8,128)} custom-call(f32[8,2,16,512]{3,2,1,0:T(8,128)} %all_to_all.11.r_ref, f32[32,64]{1,0:T(8,128)} %bitcast.9, f32[32,64]{1,0:T(8,128)} %bitcast.11, f32[8,4096]{1,0:T(8,128)} %phase_ref.3), custom_call_target="tpu_custom_call" | custom-call | tf_op jit(solution)/shard_map/pallas_call | solution.py:312
Async XLA Ops:
  27.9 12.8 %copy-start = (f32[8,2,16,512]{3,2,1,0:T(8,128)}, f32[8,2,16,512]{3,2,1,0:T(8,128)S(1)}, u32[]{:S(2)}) copy-start(f32[8,2,16,512]{3,2,1,0:T(8,128)S(1)} %all_to_all.10.own_ref) | copy-start | bytes 1572868
  27.9 11.6 %collective-permute-start.1 = (f32[8,2,16,512]{3,2,1,0:T(8,128)S(1)}, f32[8,2,16,512]{3,2,1,0:T(8,128)S(1)}, u32[]{:S(2)}, u32[]{:S(2)}) collective-permute-start(f32[8,2,16,512]{3,2,1,0:T(8,128)S(1)} %all_to_all.10.own_ref), channel_id=1, source_target_pairs={{8,0},{16,8},{24,16},{9,1},{17,9},{25,17},{10,2},{18,10},{26,18},{... | collective-permute-start | bytes 1572872 | tf_op jit(solution)/shard_map/ppermute | solution.py:297
  31.6 9.1 %collective-permute-start = (f32[8,2,16,512]{3,2,1,0:T(8,128)S(1)}, f32[8,2,16,512]{3,2,1,0:T(8,128)S(1)}, u32[]{:S(2)}, u32[]{:S(2)}) collective-permute-start(f32[8,2,16,512]{3,2,1,0:T(8,128)S(1)} %all_to_all.10.own_ref), channel_id=1, source_target_pairs={{0,8},{8,16},{16,24},{1,9},{9,17},{17,25},{2,10},{10,18},{18,26},{... | collective-permute-start | bytes 1572872 | tf_op jit(solution)/shard_map/ppermute | solution.py:296
  39.5 1.2 %copy-start.1 = (f32[8,2,16,512]{3,2,1,0:T(8,128)}, f32[8,2,16,512]{3,2,1,0:T(8,128)S(1)}, u32[]{:S(2)}) copy-start(f32[8,2,16,512]{3,2,1,0:T(8,128)S(1)} %collective-permute-done.1.after_ref) | copy-start | bytes 1572868
  40.7 0.8 %copy-start.2 = (f32[8,2,16,512]{3,2,1,0:T(8,128)}, f32[8,2,16,512]{3,2,1,0:T(8,128)S(1)}, u32[]{:S(2)}) copy-start(f32[8,2,16,512]{3,2,1,0:T(8,128)S(1)} %collective-permute-done.before_ref) | copy-start | bytes 1572868
where the time goes:
time: 70.1 us; the launch traced here: 69.8 us
  blocking collectives  34.5 us (49%)
  Pallas kernels  21.6 us (31%)
  starting transfers between devices  6.71 us (10%)
  waiting for transfers between devices  6.1 us (9%)
  local copies, waits for them, and re-layouts  0.8 us (1%)
    all_to_all x1, blocking collectives, per_device(): own = lax.all_to_all(summed, 'mem', split_axis=0, concat_axis=0, tiled=True)  20.1 us
    all_to_all x1, blocking collectives, per_device(): lax.all_to_all(incoming, 'mem', split_axis=0, concat_axis=0, tiled=True)  14.4 us
    pallas_call x1, Pallas kernels, per_device(): call(disaggregate_kernel, out_shape=jax.ShapeDtypeStruct((2, coarse_t, gr...  8.39 us
    pallas_call x1, Pallas kernels, per_device(): call(aggregate_kernel, out_shape=block, in_specs=[vmem()] * 4, out_specs=...  7.81 us
    pallas_call x1, Pallas kernels, per_device(): call(translate_kernel, out_shape=block, in_specs=[smem()] * 4 + [vmem()]...  5.42 us
    ppermute x1, waiting for transfers between devices, per_device(): after = lax.ppermute(own, 'grp', [(j, i) for i, j in up])  4.92 us
    ppermute x1, starting transfers between devices, per_device(): after = lax.ppermute(own, 'grp', [(j, i) for i, j in up])  3.69 us
    ppermute x1, starting transfers between devices, per_device(): before = lax.ppermute(own, 'grp', up)  3.02 us
  transfers between devices with their start and end apart: 2, of which 2 were waited for; matrix products, arithmetic and copies ran while one was open for 0% of the time, Pallas kernels for 0%

commit v1 on v0

v1 whole, which is shorter than its diff:
```python
import functools

import jax
import jax.numpy as jnp
from jax import lax
from jax.experimental import pallas as pl
from jax.experimental.pallas import tpu as pltpu
from jax.sharding import PartitionSpec as P

f32 = jnp.float32
bf16 = jnp.bfloat16
SUB = 8
BLOCK = 256
UNROLL = 4
COST = 50_000_000
VMEM_LIMIT = 20 << 20


def split(x):
    hi = x.astype(bf16)
    lo = (x - hi.astype(f32)).astype(bf16)
    return hi, lo


def mm(a, b):
    return jnp.dot(a, b, preferred_element_type=f32)


def mm_tn(a, b):
    return lax.dot_general(a, b, (((0,), (0,)), ((), ())), preferred_element_type=f32)


def iota(shape, dim):
    return lax.broadcasted_iota(jnp.int32, shape, dim)


def picker(shape, test):
    return jnp.where(test(iota(shape, 0), iota(shape, 1)), 1.0, 0.0).astype(bf16)


def sincos(q):
    r = q * 0.5
    z = r * r
    s = 1.0 / 6227020800.0
    for c in (-1.0 / 39916800.0, 1.0 / 362880.0, -1.0 / 5040.0, 1.0 / 120.0, -1.0 / 6.0, 1.0):
        s = s * z + c
    s = s * r
    k = 1.0 / 479001600.0
    for c in (-1.0 / 3628800.0, 1.0 / 40320.0, -1.0 / 720.0, 1.0 / 24.0, -0.5, 1.0):
        k = k * z + c
    return 2.0 * s * k, 1.0 - 2.0 * s * s


def plan(fine, members):
    per_member = fine // members
    chunks = max(1, per_member // BLOCK)
    return chunks, fine // BLOCK // chunks


def aggregate_kernel(x_ref, theta_ref, phi_ref, phase_ref, o_ref, mid_ref, cos_ref, sin_ref, *, chunk, chunks):
    coarse_t, fine_t = theta_ref.shape
    coarse_p, fine_p = phi_ref.shape
    groups = coarse_p // SUB
    span = BLOCK // fine_p
    per_member = o_ref.shape[3]
    waves = o_ref.shape[2]
    branch = phase_ref.shape[0]
    columns = branch * waves
    kept = fine_t // chunks

    chosen = picker((fine_t, kept), lambda r, c: r == (c // span * chunks + chunk) * span + c % span)
    spread_t = picker((coarse_t, coarse_t * SUB), lambda r, c: r == c // SUB)
    big = (kept * SUB, coarse_t * SUB)
    keep = iota(big, 0) % SUB == iota(big, 1) % SUB

    def theta_block(part):
        rows = mm_tn(mm(part, chosen).astype(bf16), spread_t)
        rows = jnp.broadcast_to(rows[:, None, :], (kept, SUB, coarse_t * SUB)).reshape(big)
        return jnp.where(keep, rows, 0.0).astype(bf16)

    th, tl = split(theta_ref[...])
    kh, kl = theta_block(th), theta_block(tl)
    weights = jnp.concatenate([kh, kh, kl], axis=1)

    spread_p = picker((fine_p, BLOCK), lambda r, c: r == c % fine_p)
    small = (span * coarse_p, BLOCK)
    diag = iota(small, 0) // coarse_p == iota(small, 1) // fine_p

    def phi_block(part):
        rows = mm(part, spread_p)
        rows = jnp.concatenate([rows] * span, axis=0)
        return jnp.where(diag, rows, 0.0).astype(bf16)

    ph, pl_ = split(phi_ref[...])
    bh, bl = phi_block(ph), phi_block(pl_)
    phi_weights = jnp.concatenate([bh, bh, bl], axis=0)

    sine, cosine = sincos(phase_ref[...])
    cos_ref[...] = cosine
    sin_ref[...] = sine

    for g in range(groups):
        parts = [x_ref[c, :, g].reshape(coarse_t * SUB, columns) for c in range(2)]
        hi, lo = split(jnp.concatenate(parts, axis=1))
        middle = mm(weights, jnp.concatenate([hi, lo, hi], axis=0))
        mid_ref[:, g] = middle.reshape(kept, SUB, 2 * columns)

    unit = min(BLOCK, per_member)

    def body(step, carry):
        rows = mid_ref[pl.ds(step * span, span)].reshape(span * coarse_p, 2 * columns)
        hi, lo = split(rows.T)
        fine = mm(jnp.concatenate([hi, lo, hi], axis=1), phi_weights)
        real = fine[:columns].reshape(branch, waves, BLOCK)
        imag = fine[columns:].reshape(branch, waves, BLOCK)
        lanes = pl.ds(pl.multiple_of((step * chunks + chunk) * BLOCK, BLOCK), BLOCK)
        c = cos_ref[:, lanes][:, None, :]
        s = sin_ref[:, lanes][:, None, :]
        out_real = jnp.sum(real * c - imag * s, axis=0)
        out_imag = jnp.sum(imag * c + real * s, axis=0)
        for piece in range(BLOCK // unit):
            here = slice(piece * unit, (piece + 1) * unit)
            member = step * (BLOCK // unit) + piece
            o_ref[member, 0] = out_real[:, here]
            o_ref[member, 1] = out_imag[:, here]
        return carry

    lax.fori_loop(0, kept // span, body, 0)


def translate_kernel(source_ref, kind_ref, count_ref, base_ref, factor_ref, own_ref, before_ref, after_ref, o_ref, all_ref, *, chunk):
    members = own_ref.shape[0]
    targets, slots = source_ref.shape
    for i, ref in enumerate((before_ref, own_ref, after_ref)):
        all_ref[pl.ds(i * members, members)] = ref[...]
    base = base_ref[0]
    waves, directions = o_ref.shape[2:]
    lanes = pl.ds(chunk * directions, directions)

    def target_body(t, carry):
        count = count_ref[t]

        def slot_body(step, acc):
            real, imag = acc
            for i in range(UNROLL):
                k = step * UNROLL + i
                live = k < count
                at = jnp.where(live, source_ref[t, k] - base, 0)
                kind = jnp.where(live, kind_ref[t, k], 0)
                weight = jnp.where(live, 1.0, 0.0).astype(f32)
                factor = factor_ref[kind, :, lanes] * weight
                fr = factor[0:1]
                fi = factor[1:2]
                sr = all_ref[at, 0]
                si = all_ref[at, 1]
                real = real + (fr * sr - fi * si)
                imag = imag + (fr * si + fi * sr)
            return real, imag

        zero = jnp.zeros((waves, directions), f32)
        real, imag = lax.fori_loop(0, (count + UNROLL - 1) // UNROLL, slot_body, (zero, zero))
        o_ref[t, 0] = real
        o_ref[t, 1] = imag
        return carry

    lax.fori_loop(0, targets, target_body, 0)


def disaggregate_kernel(*refs, chunk, chunks, first):
    if first:
        r_ref, theta_ref, phi_ref, phase_ref, o_ref, mid_ref, cos_ref, sin_ref = refs
    else:
        r_ref, theta_ref, phi_ref, phase_ref, partial_ref, o_ref, mid_ref, cos_ref, sin_ref = refs
    coarse_t, fine_t = theta_ref.shape
    coarse_p, fine_p = phi_ref.shape
    groups = coarse_p // SUB
    span = BLOCK // fine_p
    per_member = r_ref.shape[3]
    waves = r_ref.shape[2]
    branch = phase_ref.shape[0]
    columns = branch * waves
    kept = fine_t // chunks

    def source_row(c):
        a = c // SUB
        return (a // span * chunks + chunk) * span + a % span

    spread_t = picker((fine_t, kept * SUB), lambda r, c: r == source_row(c))
    big = (coarse_t * SUB, kept * SUB)
    keep = iota(big, 0) % SUB == iota(big, 1) % SUB

    def theta_block(part):
        rows = mm(part, spread_t)
        rows = jnp.broadcast_to(rows[:, None, :], (coarse_t, SUB, kept * SUB)).reshape(big)
        return jnp.where(keep, rows, 0.0).astype(bf16)

    th, tl = split(theta_ref[...])
    kh, kl = theta_block(th), theta_block(tl)
    weights = jnp.concatenate([kh, kh, kl], axis=1)

    narrow = span * coarse_p
    spread_p = picker((coarse_p, narrow), lambda r, c: r == c % coarse_p)
    small = (BLOCK, narrow)
    diag = iota(small, 0) // fine_p == iota(small, 1) // coarse_p

    def phi_block(part):
        rows = mm_tn(part, spread_p)
        rows = jnp.concatenate([rows] * span, axis=0)
        return jnp.where(diag, rows, 0.0).astype(bf16)

    ph, pl_ = split(phi_ref[...])
    phi_weights = jnp.concatenate([phi_block(ph), phi_block(pl_)], axis=1)

    sine, cosine = sincos(phase_ref[...])
    cos_ref[...] = cosine
    sin_ref[...] = sine
    unit = min(BLOCK, per_member)

    def body(step, carry):
        many = BLOCK // unit
        parts = [[r_ref[step * many + piece, c] for piece in range(many)] for c in range(2)]
        real, imag = [jnp.concatenate(p, axis=1)[None] for p in parts]
        lanes = pl.ds(pl.multiple_of((step * chunks + chunk) * BLOCK, BLOCK), BLOCK)
        c = cos_ref[:, lanes][:, None, :]
        s = sin_ref[:, lanes][:, None, :]
        local = jnp.concatenate(
            [
                (real * c + imag * s).reshape(columns, BLOCK),
                (imag * c - real * s).reshape(columns, BLOCK),
            ],
            axis=0,
        )
        hi, lo = split(local)
        y = mm(jnp.concatenate([hi, lo], axis=0), phi_weights)
        rows = 2 * columns
        folded = y[:rows, :narrow] + (y[rows:, :narrow] + y[:rows, narrow:])
        mid_ref[pl.ds(step * span, span)] = folded.T.reshape(span, groups, SUB, rows)
        return carry

    lax.fori_loop(0, kept // span, body, 0)

    for g in range(groups):
        hi, lo = split(mid_ref[:, g].reshape(kept * SUB, 2 * columns))
        coarse = mm(weights, jnp.concatenate([hi, lo, hi], axis=0))
        for c in range(2):
            part = coarse[:, c * columns : (c + 1) * columns].reshape(coarse_t, SUB, columns)
            o_ref[c, :, g] = part if first else part + partial_ref[c, :, g]


def vmem():
    return pl.BlockSpec(memory_space=pltpu.VMEM)


def smem():
    return pl.BlockSpec(memory_space=pltpu.SMEM)


def per_device(
    child_field,
    theta_interp,
    phi_interp,
    child_phase,
    translation,
    inter_source,
    inter_kind,
    inter_count,
    *,
    interpret=False,
):
    call = functools.partial(
        pl.pallas_call,
        interpret=interpret,
        out_specs=vmem(),
        compiler_params=pltpu.CompilerParams(vmem_limit_bytes=VMEM_LIMIT),
    )
    branch, fine = child_phase.shape
    columns = child_field.shape[2]
    waves = columns // branch
    fine_t, coarse_t = theta_interp.shape
    coarse_p = phi_interp.shape[1]
    groups = coarse_p // SUB
    members = lax.axis_size("mem")
    grp_count = lax.axis_size("grp")
    chunks, steps = plan(fine, members)
    width = fine // members // chunks
    theta_t = theta_interp.T
    phi_t = phi_interp.T
    factors = jnp.transpose(translation, (1, 0, 2))
    scratch = [
        pltpu.VMEM((fine_t // chunks, groups, SUB, 2 * columns), f32),
        pltpu.VMEM((branch, fine), f32),
        pltpu.VMEM((branch, fine), f32),
    ]
    block = jax.ShapeDtypeStruct((members, 2, waves, width), f32)
    field = child_field.reshape(2, coarse_t, groups, SUB, columns)
    base = ((lax.axis_index("grp") - 1) * members).astype(jnp.int32).reshape(1)
    up = [(i, i + 1) for i in range(grp_count - 1)]
    down = [(j, i) for i, j in up]

    def exchange(x):
        return lax.all_to_all(x, "mem", split_axis=0, concat_axis=0, tiled=True)

    received = []
    for h in range(chunks):
        summed = call(
            functools.partial(aggregate_kernel, chunk=h, chunks=chunks),
            out_shape=block,
            in_specs=[vmem()] * 4,
            scratch_shapes=scratch,
            name=f"aggregate{h}",
            cost_estimate=pl.CostEstimate(flops=COST, transcendentals=0, bytes_accessed=1 << 20),
        )(field, theta_t, phi_t, child_phase)
        received.append(exchange(summed))
    returned = []
    for h in range(chunks):
        own = received[h]
        incoming = call(
            functools.partial(translate_kernel, chunk=h),
            out_shape=block,
            in_specs=[smem()] * 4 + [vmem()] * 4,
            scratch_shapes=[pltpu.VMEM((3 * members, 2, waves, width), f32)],
            name=f"translate{h}",
            cost_estimate=pl.CostEstimate(flops=COST, transcendentals=0, bytes_accessed=1 << 20),
        )(inter_source, inter_kind, inter_count, base, factors, own, lax.ppermute(own, "grp", up), lax.ppermute(own, "grp", down))
        returned.append(exchange(incoming))
    out = None
    for h in range(chunks):
        first = h == 0
        out = call(
            functools.partial(disaggregate_kernel, chunk=h, chunks=chunks, first=first),
            out_shape=jax.ShapeDtypeStruct(field.shape, f32),
            in_specs=[vmem()] * (4 if first else 5),
            scratch_shapes=scratch,
            name=f"disaggregate{h}",
            cost_estimate=pl.CostEstimate(flops=COST, transcendentals=0, bytes_accessed=1 << 20),
        )(*((returned[h], theta_t, phi_t, child_phase) + (() if first else (out,))))
    return out.reshape(child_field.shape)


def solution(mesh):
    return jax.shard_map(
        per_device,
        mesh=mesh,
        in_specs=(
            P(None, None, ("grp", "mem")),
            P(),
            P(),
            P(),
            P(None, None, "mem"),
            P("grp", None),
            P("grp", None),
            P("grp"),
        ),
        out_specs=P(None, None, ("grp", "mem")),
        check_vma=False,
    )
```

time: 70.1 us -> 76.1 us (1.086)
  the two profiles are of different devices: /device:TPU:1 before, /device:TPU:2 now
where the time goes in v1:
time: 76.1 us; the launch traced here: 75.4 us
  starting transfers between devices  30.2 us (40%)
  Pallas kernels  21.2 us (28%)
  waiting for transfers between devices  20.3 us (27%)
  local copies, waits for them, and re-layouts  3.59 us (5%)
    all_to_all x4, starting transfers between devices, exchange(): return lax.all_to_all(x, 'mem', split_axis=0, concat_axis=0, tiled=True)  21.6 us
    all_to_all x4, waiting for transfers between devices, exchange(): return lax.all_to_all(x, 'mem', split_axis=0, concat_axis=0, tiled=True)  9.75 us
    pallas_call x2, Pallas kernels, per_device(): call(functools.partial(aggregate_kernel, chunk=h, chunks=chunks), out_sha...  8.09 us
    ppermute x2, waiting for transfers between devices, per_device(): lax.ppermute(own, 'grp', up)  7.64 us
    pallas_call x2, Pallas kernels, per_device(): call(functools.partial(disaggregate_kernel, chunk=h, chunks=chunks, first...  7.61 us
    pallas_call x2, Pallas kernels, per_device(): call(functools.partial(translate_kernel, chunk=h), out_shape=block, in_sp...  5.46 us
    ppermute x2, starting transfers between devices, per_device(): lax.ppermute(own, 'grp', up)  4.84 us
    ppermute x2, starting transfers between devices, per_device(): lax.ppermute(own, 'grp', down)  3.82 us
  transfers between devices with their start and end apart: 8, of which 6 were waited for; matrix products, arithmetic and copies ran while one was open for 0% of the time, Pallas kernels for 17%

profile of v1, /device:TPU:2, one launch (start us, length us, event | category | flops | bytes accessed | tf_op | source)
XLA Modules:
  0.0 75.4 jit_solution(11665781060282940410)
XLA Ops:
  0.0 0.0 copy-start.1
  0.0 1.2 %copy-done.1 = f32[2,1024,128]{2,1,0:T(8,128)S(1)} copy-done((f32[2,1024,128]{2,1,0:T(8,128)S(1)}, f32[2,1024,128]{2,1,0:T(8,128)}, u32[]{:S(2)}) %copy-start.1) | copy-done | bytes 1048600
  1.2 0.0 copy-start.3
  1.2 0.9 %copy-done.3 = f32[8,4096]{1,0:T(8,128)S(1)} copy-done((f32[8,4096]{1,0:T(8,128)S(1)}, f32[8,4096]{1,0:T(8,128)}, u32[]{:S(2)}) %copy-start.3) | copy-done | bytes 131096
  2.1 0.0 copy-start.5
  2.1 0.7 copy-done.5
  2.8 0.0 copy-start.7
  2.9 0.7 copy-done.7
  3.6 0.0 copy-start.2
  3.6 0.0 copy-start.4
  3.6 0.0 copy-start.6
  3.6 0.0 copy-start.8
  3.6 4.0 %aggregate0.1 = f32[8,2,16,256]{3,2,1,0:T(8,128)} custom-call(f32[2,32,4,8,128]{4,3,2,1,0:T(8,128)S(1)} %bitcast.8, f32[32,64]{1,0:T(8,128)S(1)} %bitcast.10, f32[32,64]{1,0:T(8,128)S(1)} %bitcast.14, f32[8,4096]{1,0:T(8,128)S(1)} %copy-done.3), custom_call_target="tpu_custom_call" | custom-call | flops 50000000 | bytes 1048576 | tf_op jit(solution)/shard_map/aggregate0/pallas_call | solution.py:305
  7.6 0.0 copy-start
  7.6 0.0 copy-start.9
  7.6 0.0 copy-start.10
  7.6 0.0 copy-start.11
  7.6 6.0 %all-to-all-start.2 = ((f32[8,2,16,256]{3,2,1,0:T(8,128)}), f32[8,2,16,256]{3,2,1,0:T(8,128)S(1)}, u32[]{:S(2)}, u32[]{:S(2)}) async-start(f32[8,2,16,256]{3,2,1,0:T(8,128)} %aggregate0.1), calls=%async_computation.2 | async-start | bytes 524288 | tf_op jit(solution)/shard_map/all_to_all | solution.py:301
  13.6 0.0 copy-done.2
  13.6 0.0 copy-done.4
  13.6 0.0 copy-done.6
  13.6 0.0 copy-done.8
  13.6 4.0 %aggregate1.1 = f32[8,2,16,256]{3,2,1,0:T(8,128)} custom-call(f32[2,32,4,8,128]{4,3,2,1,0:T(8,128)S(1)} %bitcast.9, f32[32,64]{1,0:T(8,128)S(1)} %bitcast.11, f32[32,64]{1,0:T(8,128)S(1)} %bitcast.15, f32[8,4096]{1,0:T(8,128)S(1)} %copy-done.4), custom_call_target="tpu_custom_call" | custom-call | flops 50000000 | bytes 1048576 | tf_op jit(solution)/shard_map/aggregate1/pallas_call | solution.py:305
  17.7 4.8 %all-to-all-done.2.own_ref = f32[8,2,16,256]{3,2,1,0:T(8,128)S(1)} async-done(((f32[8,2,16,256]{3,2,1,0:T(8,128)}), f32[8,2,16,256]{3,2,1,0:T(8,128)S(1)}, u32[]{:S(2)}, u32[]{:S(2)}) %all-to-all-start.2) | async-done | bytes 262176 | tf_op jit(solution)/shard_map/all_to_all | solution.py:301
  22.5 3.6 %all-to-all-start = ((f32[8,2,16,256]{3,2,1,0:T(8,128)}), f32[8,2,16,256]{3,2,1,0:T(8,128)S(1)}, u32[]{:S(2)}, u32[]{:S(2)}) async-start(f32[8,2,16,256]{3,2,1,0:T(8,128)} %aggregate1.1), calls=%async_computation | async-start | bytes 524288 | tf_op jit(solution)/shard_map/all_to_all | solution.py:301
  26.1 1.9 %collective-permute-start.3 = (f32[8,2,16,256]{3,2,1,0:T(8,128)S(1)}, f32[8,2,16,256]{3,2,1,0:T(8,128)S(1)}, u32[]{:S(2)}, u32[]{:S(2)}) collective-permute-start(f32[8,2,16,256]{3,2,1,0:T(8,128)S(1)} %all-to-all-done.2.own_ref), channel_id=1, source_target_pairs={{8,0},{16,8},{24,16},{9,1},{17,9},{25,17},{10,2},{18,10},{26,18},{... | collective-permute-start | bytes 786440 | tf_op jit(solution)/shard_map/ppermute | solution.py:324
  28.0 2.4 %collective-permute-start.2 = (f32[8,2,16,256]{3,2,1,0:T(8,128)S(1)}, f32[8,2,16,256]{3,2,1,0:T(8,128)S(1)}, u32[]{:S(2)}, u32[]{:S(2)}) collective-permute-start(f32[8,2,16,256]{3,2,1,0:T(8,128)S(1)} %all-to-all-done.2.own_ref), channel_id=1, source_target_pairs={{0,8},{8,16},{16,24},{1,9},{9,17},{17,25},{2,10},{10,18},{18,26},{... | collective-permute-start | bytes 786440 | tf_op jit(solution)/shard_map/ppermute | solution.py:324
  30.5 1.4 %collective-permute-done.3.after_ref = f32[8,2,16,256]{3,2,1,0:T(8,128)S(1)} collective-permute-done((f32[8,2,16,256]{3,2,1,0:T(8,128)S(1)}, f32[8,2,16,256]{3,2,1,0:T(8,128)S(1)}, u32[]{:S(2)}, u32[]{:S(2)}) %collective-permute-start.3) | collective-permute-done | bytes 262176 | tf_op jit(solution)/shard_map/ppermute | solution.py:324
  31.9 3.8 %collective-permute-done.2.before_ref = f32[8,2,16,256]{3,2,1,0:T(8,128)S(1)} collective-permute-done((f32[8,2,16,256]{3,2,1,0:T(8,128)S(1)}, f32[8,2,16,256]{3,2,1,0:T(8,128)S(1)}, u32[]{:S(2)}, u32[]{:S(2)}) %collective-permute-start.2) | collective-permute-done | bytes 262176 | tf_op jit(solution)/shard_map/ppermute | solution.py:324
  35.7 0.0 copy-done
  35.7 0.0 copy-done.9
  35.7 0.0 copy-done.10
  35.7 0.0 copy-done.11
  35.7 2.7 %translate0.1 = f32[8,2,16,256]{3,2,1,0:T(8,128)} custom-call(s32[8,24]{1,0:T(8,128)S(1)} %copy-done.9, s32[8,24]{1,0:T(8,128)S(1)} %copy-done.10, s32[8]{0:T(128)S(1)} %copy-done.11, s32[1]{0:T(128)} %bitcast.base_ref, f32[316,2,512]{2,1,0:T(2,128)S(1)} %bitcast.6, f32[8,2,16,256]{3,2,1,0:T(8,128)S(1)} %all-to-all-done.2.own_ref, ...), custom_call_target="tpu_custom_call" | custom-call | flops 50000000 | bytes 1048576 | tf_op jit(solution)/shard_map/translate0/pallas_call | solution.py:317
  38.5 0.0 all-to-all-done.own_ref
  38.5 6.0 %all-to-all-start.3 = ((f32[8,2,16,256]{3,2,1,0:T(8,128)}), f32[8,2,16,256]{3,2,1,0:T(8,128)S(1)}, u32[]{:S(2)}, u32[]{:S(2)}) async-start(f32[8,2,16,256]{3,2,1,0:T(8,128)} %translate0.1), calls=%async_computation.3 | async-start | bytes 524288 | tf_op jit(solution)/shard_map/all_to_all | solution.py:301
  44.5 1.9 %collective-permute-start.1 = (f32[8,2,16,256]{3,2,1,0:T(8,128)S(1)}, f32[8,2,16,256]{3,2,1,0:T(8,128)S(1)}, u32[]{:S(2)}, u32[]{:S(2)}) collective-permute-start(f32[8,2,16,256]{3,2,1,0:T(8,128)S(1)} %all-to-all-done.own_ref), channel_id=1, source_target_pairs={{8,0},{16,8},{24,16},{9,1},{17,9},{25,17},{10,2},{18,10},{26,18},{... | collective-permute-start | bytes 786440 | tf_op jit(solution)/shard_map/ppermute | solution.py:324
  46.4 2.4 %collective-permute-start = (f32[8,2,16,256]{3,2,1,0:T(8,128)S(1)}, f32[8,2,16,256]{3,2,1,0:T(8,128)S(1)}, u32[]{:S(2)}, u32[]{:S(2)}) collective-permute-start(f32[8,2,16,256]{3,2,1,0:T(8,128)S(1)} %all-to-all-done.own_ref), channel_id=1, source_target_pairs={{0,8},{8,16},{16,24},{1,9},{9,17},{17,25},{2,10},{10,18},{18,26},{... | collective-permute-start | bytes 786440 | tf_op jit(solution)/shard_map/ppermute | solution.py:324
  48.8 1.4 %collective-permute-done.1.after_ref = f32[8,2,16,256]{3,2,1,0:T(8,128)S(1)} collective-permute-done((f32[8,2,16,256]{3,2,1,0:T(8,128)S(1)}, f32[8,2,16,256]{3,2,1,0:T(8,128)S(1)}, u32[]{:S(2)}, u32[]{:S(2)}) %collective-permute-start.1) | collective-permute-done | bytes 262176 | tf_op jit(solution)/shard_map/ppermute | solution.py:324
  50.3 3.8 %collective-permute-done.before_ref = f32[8,2,16,256]{3,2,1,0:T(8,128)S(1)} collective-permute-done((f32[8,2,16,256]{3,2,1,0:T(8,128)S(1)}, f32[8,2,16,256]{3,2,1,0:T(8,128)S(1)}, u32[]{:S(2)}, u32[]{:S(2)}) %collective-permute-start) | collective-permute-done | bytes 262176 | tf_op jit(solution)/shard_map/ppermute | solution.py:324
  54.1 2.7 %translate1.1 = f32[8,2,16,256]{3,2,1,0:T(8,128)} custom-call(s32[8,24]{1,0:T(8,128)S(1)} %copy-done.9, s32[8,24]{1,0:T(8,128)S(1)} %copy-done.10, s32[8]{0:T(128)S(1)} %copy-done.11, s32[1]{0:T(128)} %bitcast.base_ref, f32[316,2,512]{2,1,0:T(2,128)S(1)} %bitcast.7, f32[8,2,16,256]{3,2,1,0:T(8,128)S(1)} %all-to-all-done.own_ref, ...), custom_call_target="tpu_custom_call" | custom-call | flops 50000000 | bytes 1048576 | tf_op jit(solution)/shard_map/translate1/pallas_call | solution.py:317
  56.8 0.0 all-to-all-done.3.refs_0_
  56.8 6.0 %all-to-all-start.1 = ((f32[8,2,16,256]{3,2,1,0:T(8,128)}), f32[8,2,16,256]{3,2,1,0:T(8,128)S(1)}, u32[]{:S(2)}, u32[]{:S(2)}) async-start(f32[8,2,16,256]{3,2,1,0:T(8,128)} %translate1.1), calls=%async_computation.1 | async-start | bytes 524288 | tf_op jit(solution)/shard_map/all_to_all | solution.py:301
  62.8 3.3 %disaggregate0.1.refs_4_ = f32[2,32,4,8,128]{4,3,2,1,0:T(8,128)S(1)} custom-call(f32[8,2,16,256]{3,2,1,0:T(8,128)S(1)} %all-to-all-done.3.refs_0_, f32[32,64]{1,0:T(8,128)S(1)} %bitcast.12, f32[32,64]{1,0:T(8,128)S(1)} %bitcast.16, f32[8,4096]{1,0:T(8,128)S(1)} %copy-done.4), custom_call_target="tpu_custom_call" | custom-call | flops 50000000 | bytes 1048576 | tf_op jit(solution)/shard_map/disaggregate0/pallas_call | solution.py:329
  66.1 4.9 %all-to-all-done.1.refs_0_ = f32[8,2,16,256]{3,2,1,0:T(8,128)S(1)} async-done(((f32[8,2,16,256]{3,2,1,0:T(8,128)}), f32[8,2,16,256]{3,2,1,0:T(8,128)S(1)}, u32[]{:S(2)}, u32[]{:S(2)}) %all-to-all-start.1) | async-done | bytes 262176 | tf_op jit(solution)/shard_map/all_to_all | solution.py:301
  71.0 4.3 %disaggregate1.1 = f32[2,32,4,8,128]{4,3,2,1,0:T(8,128)} custom-call(f32[8,2,16,256]{3,2,1,0:T(8,128)S(1)} %all-to-all-done.1.refs_0_, f32[32,64]{1,0:T(8,128)S(1)} %bitcast.13, f32[32,64]{1,0:T(8,128)S(1)} %bitcast.17, f32[8,4096]{1,0:T(8,128)S(1)} %copy-done.4, f32[2,32,4,8,128]{4,3,2,1,0:T(8,128)S(1)} %disaggregate0.1.refs_4_), custom_call_target="tpu_custom_call" | custom-call | flops 50000000 | bytes 1048576 | tf_op jit(solution)/shard_map/disaggregate1/pallas_call | solution.py:329
Async XLA Ops:
  0.0 1.2 %copy-start.1 = (f32[2,1024,128]{2,1,0:T(8,128)S(1)}, f32[2,1024,128]{2,1,0:T(8,128)}, u32[]{:S(2)}) copy-start(f32[2,1024,128]{2,1,0:T(8,128)} %param.8) | copy-start | bytes 3145732
  1.2 0.9 %copy-start.3 = (f32[8,4096]{1,0:T(8,128)S(1)}, f32[8,4096]{1,0:T(8,128)}, u32[]{:S(2)}) copy-start(f32[8,4096]{1,0:T(8,128)} %refs_3_.3) | copy-start | bytes 393220
  2.1 0.7 copy-start.5
  2.8 0.7 copy-start.7
  3.6 10.0 %copy-start.2 = (f32[2,1024,128]{2,1,0:T(8,128)S(1)}, f32[2,1024,128]{2,1,0:T(8,128)}, u32[]{:S(2)}) copy-start(f32[2,1024,128]{2,1,0:T(8,128)} %param.8) | copy-start | bytes 3145732
  3.6 10.0 %copy-start.4 = (f32[8,4096]{1,0:T(8,128)S(1)}, f32[8,4096]{1,0:T(8,128)}, u32[]{:S(2)}) copy-start(f32[8,4096]{1,0:T(8,128)} %refs_3_.3) | copy-start | bytes 393220
  3.6 10.1 %copy-start.6 = (f32[64,32]{0,1:T(8,128)S(1)}, f32[64,32]{0,1:T(8,128)}, u32[]{:S(2)}) copy-start(f32[64,32]{0,1:T(8,128)} %param.9) | copy-start | bytes 24580
  3.6 10.1 %copy-start.8 = (f32[64,32]{0,1:T(8,128)S(1)}, f32[64,32]{0,1:T(8,128)}, u32[]{:S(2)}) copy-start(f32[64,32]{0,1:T(8,128)} %param.10) | copy-start | bytes 24580
  7.6 28.1 %copy-start = (f32[2,316,512]{2,0,1:T(2,128)S(1)}, f32[2,316,512]{2,0,1:T(2,128)}, u32[]{:S(2)}) copy-start(f32[2,316,512]{2,0,1:T(2,128)} %param.12) | copy-start | bytes 3883012
  7.6 28.1 %copy-start.9 = (s32[8,24]{1,0:T(8,128)S(1)}, s32[8,24]{1,0:T(8,128)}, u32[]{:S(2)}) copy-start(s32[8,24]{1,0:T(8,128)} %source_ref.3) | copy-start | bytes 2308
  7.6 28.1 %copy-start.10 = (s32[8,24]{1,0:T(8,128)S(1)}, s32[8,24]{1,0:T(8,128)}, u32[]{:S(2)}) copy-start(s32[8,24]{1,0:T(8,128)} %kind_ref.3) | copy-start | bytes 2308
  7.6 28.1 %copy-start.11 = (s32[8]{0:T(128)S(1)}, s32[8]{0:T(128)}, u32[]{:S(2)}) copy-start(s32[8]{0:T(128)} %count_ref.3) | copy-start | bytes 100
  7.6 14.9 %all-to-all-start.2 = ((f32[8,2,16,256]{3,2,1,0:T(8,128)}), f32[8,2,16,256]{3,2,1,0:T(8,128)S(1)}, u32[]{:S(2)}, u32[]{:S(2)}) async-start(f32[8,2,16,256]{3,2,1,0:T(8,128)} %aggregate0.1), calls=%async_computation.2 | async-start | bytes 524288 | tf_op jit(solution)/shard_map/all_to_all | solution.py:301
  22.5 15.9 %all-to-all-start = ((f32[8,2,16,256]{3,2,1,0:T(8,128)}), f32[8,2,16,256]{3,2,1,0:T(8,128)S(1)}, u32[]{:S(2)}, u32[]{:S(2)}) async-start(f32[8,2,16,256]{3,2,1,0:T(8,128)} %aggregate1.1), calls=%async_computation | async-start | bytes 524288 | tf_op jit(solution)/shard_map/all_to_all | solution.py:301
  26.1 5.8 %collective-permute-start.3 = (f32[8,2,16,256]{3,2,1,0:T(8,128)S(1)}, f32[8,2,16,256]{3,2,1,0:T(8,128)S(1)}, u32[]{:S(2)}, u32[]{:S(2)}) collective-permute-start(f32[8,2,16,256]{3,2,1,0:T(8,128)S(1)} %all-to-all-done.2.own_ref), channel_id=1, source_target_pairs={{8,0},{16,8},{24,16},{9,1},{17,9},{25,17},{10,2},{18,10},{26,18},{... | collective-permute-start | bytes 786440 | tf_op jit(solution)/shard_map/ppermute | solution.py:324
  28.0 7.7 %collective-permute-start.2 = (f32[8,2,16,256]{3,2,1,0:T(8,128)S(1)}, f32[8,2,16,256]{3,2,1,0:T(8,128)S(1)}, u32[]{:S(2)}, u32[]{:S(2)}) collective-permute-start(f32[8,2,16,256]{3,2,1,0:T(8,128)S(1)} %all-to-all-done.2.own_ref), channel_id=1, source_target_pairs={{0,8},{8,16},{16,24},{1,9},{9,17},{17,25},{2,10},{10,18},{18,26},{... | collective-permute-start | bytes 786440 | tf_op jit(solution)/shard_map/ppermute | solution.py:324
  38.5 18.3 %all-to-all-start.3 = ((f32[8,2,16,256]{3,2,1,0:T(8,128)}), f32[8,2,16,256]{3,2,1,0:T(8,128)S(1)}, u32[]{:S(2)}, u32[]{:S(2)}) async-start(f32[8,2,16,256]{3,2,1,0:T(8,128)} %translate0.1), calls=%async_computation.3 | async-start | bytes 524288 | tf_op jit(solution)/shard_map/all_to_all | solution.py:301
  44.5 5.8 %collective-permute-start.1 = (f32[8,2,16,256]{3,2,1,0:T(8,128)S(1)}, f32[8,2,16,256]{3,2,1,0:T(8,128)S(1)}, u32[]{:S(2)}, u32[]{:S(2)}) collective-permute-start(f32[8,2,16,256]{3,2,1,0:T(8,128)S(1)} %all-to-all-done.own_ref), channel_id=1, source_target_pairs={{8,0},{16,8},{24,16},{9,1},{17,9},{25,17},{10,2},{18,10},{26,18},{... | collective-permute-start | bytes 786440 | tf_op jit(solution)/shard_map/ppermute | solution.py:324
  46.4 7.7 %collective-permute-start = (f32[8,2,16,256]{3,2,1,0:T(8,128)S(1)}, f32[8,2,16,256]{3,2,1,0:T(8,128)S(1)}, u32[]{:S(2)}, u32[]{:S(2)}) collective-permute-start(f32[8,2,16,256]{3,2,1,0:T(8,128)S(1)} %all-to-all-done.own_ref), channel_id=1, source_target_pairs={{0,8},{8,16},{16,24},{1,9},{9,17},{17,25},{2,10},{10,18},{18,26},{... | collective-permute-start | bytes 786440 | tf_op jit(solution)/shard_map/ppermute | solution.py:324
  56.8 14.2 %all-to-all-start.1 = ((f32[8,2,16,256]{3,2,1,0:T(8,128)}), f32[8,2,16,256]{3,2,1,0:T(8,128)S(1)}, u32[]{:S(2)}, u32[]{:S(2)}) async-start(f32[8,2,16,256]{3,2,1,0:T(8,128)} %translate1.1), calls=%async_computation.1 | async-start | bytes 524288 | tf_op jit(solution)/shard_map/all_to_all | solution.py:301

commit v2 on v0

v2 whole, which is shorter than its diff:
```python
import jax
import jax.numpy as jnp
from jax import lax
from jax.experimental import pallas as pl
from jax.experimental.pallas import tpu as pltpu
from jax.sharding import PartitionSpec as P

f32 = jnp.float32
bf16 = jnp.bfloat16
SUB = 8
BLOCK = 256
UNROLL = 4
PAIR = 2
COST = 50_000_000
VMEM_LIMIT = 20 << 20
VMEM_WHOLE = 60 * 1024 * 1024


def split(x):
    hi = x.astype(bf16)
    lo = (x - hi.astype(f32)).astype(bf16)
    return hi, lo


def mm(a, b):
    return jnp.dot(a, b, preferred_element_type=f32)


def mm_tn(a, b):
    return lax.dot_general(a, b, (((0,), (0,)), ((), ())), preferred_element_type=f32)


def iota(shape, dim):
    return lax.broadcasted_iota(jnp.int32, shape, dim)


def picker(shape, test):
    return jnp.where(test(iota(shape, 0), iota(shape, 1)), 1.0, 0.0).astype(bf16)


def sincos(q):
    r = q * 0.5
    z = r * r
    s = 1.0 / 6227020800.0
    for c in (-1.0 / 39916800.0, 1.0 / 362880.0, -1.0 / 5040.0, 1.0 / 120.0, -1.0 / 6.0, 1.0):
        s = s * z + c
    s = s * r
    k = 1.0 / 479001600.0
    for c in (-1.0 / 3628800.0, 1.0 / 40320.0, -1.0 / 720.0, 1.0 / 24.0, -0.5, 1.0):
        k = k * z + c
    return 2.0 * s * k, 1.0 - 2.0 * s * s


def theta_rows(part, count, spread, keep):
    rows = spread(part)
    wide = rows.shape[1]
    rows = jnp.broadcast_to(rows[:, None, :], (count, SUB, wide)).reshape(count * SUB, wide)
    return jnp.where(keep, rows, 0.0).astype(bf16)


def aggregate_kernel(x_ref, theta_ref, phi_ref, phase_ref, o_ref, x_buf, theta_buf, phi_buf, phase_buf, o_buf, mid_ref, cos_ref, sin_ref, x_sems, sems, o_sems):
    coarse_t, fine_t = theta_ref.shape
    coarse_p, fine_p = phi_ref.shape
    groups = coarse_p // SUB
    span = BLOCK // fine_p
    members, _, waves, per_member = o_ref.shape
    branch, fine = phase_ref.shape
    columns = branch * waves

    small = [
        pltpu.make_async_copy(a, b, sems.at[i])
        for i, (a, b) in enumerate(((theta_ref, theta_buf), (phi_ref, phi_buf), (phase_ref, phase_buf)))
    ]
    large = [pltpu.make_async_copy(x_ref.at[:, :, g], x_buf.at[:, :, g], x_sems.at[g]) for g in range(groups)]
    for copy in small + large:
        copy.start()
    for copy in small:
        copy.wait()

    spread_t = picker((coarse_t, coarse_t * SUB), lambda r, c: r == c // SUB)
    big = (fine_t * SUB, coarse_t * SUB)
    keep = iota(big, 0) % SUB == iota(big, 1) % SUB
    kh, kl = [theta_rows(part, fine_t, lambda p: mm_tn(p, spread_t), keep) for part in split(theta_buf[...])]
    weights = jnp.concatenate([kh, kh, kl], axis=1)

    spread_p = picker((fine_p, BLOCK), lambda r, c: r == c % fine_p)
    shape = (span * coarse_p, BLOCK)
    diag = iota(shape, 0) // coarse_p == iota(shape, 1) // fine_p

    def phi_block(part):
        rows = jnp.concatenate([mm(part, spread_p)] * span, axis=0)
        return jnp.where(diag, rows, 0.0).astype(bf16)

    bh, bl = [phi_block(part) for part in split(phi_buf[...])]
    phi_weights = jnp.concatenate([bh, bh, bl], axis=0)

    sine, cosine = sincos(phase_buf[...])
    cos_ref[...] = cosine
    sin_ref[...] = sine

    for g in range(groups):
        large[g].wait()
        parts = [x_buf[c, :, g].reshape(coarse_t * SUB, columns) for c in range(2)]
        hi, lo = split(jnp.concatenate(parts, axis=1))
        middle = mm(weights, jnp.concatenate([hi, lo, hi], axis=0))
        mid_ref[:, g] = middle.reshape(fine_t, SUB, 2 * columns)

    unit = min(BLOCK, per_member)
    batch = max(per_member, PAIR * BLOCK)
    many = batch // per_member

    def out_copy(member):
        return pltpu.make_async_copy(o_buf.at[member], o_ref.at[member], o_sems.at[member])

    def body(step, carry):
        for i in range(batch // BLOCK):
            rows = mid_ref[pl.ds((step * (batch // BLOCK) + i) * span, span)].reshape(span * coarse_p, 2 * columns)
            hi, lo = split(rows.T)
            fine_part = mm(jnp.concatenate([hi, lo, hi], axis=1), phi_weights)
            real = fine_part[:columns].reshape(branch, waves, BLOCK)
            imag = fine_part[columns:].reshape(branch, waves, BLOCK)
            lanes = pl.ds(pl.multiple_of(step * batch + i * BLOCK, BLOCK), BLOCK)
            c = cos_ref[:, lanes][:, None, :]
            s = sin_ref[:, lanes][:, None, :]
            outs = jnp.sum(real * c - imag * s, axis=0), jnp.sum(imag * c + real * s, axis=0)
            for piece in range(BLOCK // unit):
                at = i * BLOCK + piece * unit
                member = step * many + at // per_member
                there = pl.ds(at % per_member, unit)
                for part in range(2):
                    o_buf[member, part, :, there] = outs[part][:, piece * unit : (piece + 1) * unit]
        for j in range(many):
            out_copy(step * many + j).start()
        return carry

    lax.fori_loop(0, fine // batch, body, 0)

    def drain(member, carry):
        out_copy(member).wait()
        return carry

    lax.fori_loop(0, members, drain, 0)


def add_slots(entry_of, count, factor_ref, data_ref, acc, wide):
    def slot_body(step, acc):
        real, imag = acc
        for i in range(UNROLL):
            k = step * UNROLL + i
            live = k < count
            entry = jnp.where(live, entry_of(k), 0)
            kind = lax.div(entry, wide)
            at = entry - kind * wide
            factor = factor_ref[kind] * jnp.where(live, 1.0, 0.0).astype(f32)
            fr = factor[0:1]
            fi = factor[1:2]
            sr = data_ref[at, 0]
            si = data_ref[at, 1]
            real = real + (fr * sr - fi * si)
            imag = imag + (fr * si + fi * sr)
        return real, imag

    return lax.fori_loop(0, lax.div(count + (UNROLL - 1), UNROLL), slot_body, acc)


def near_kernel(source_ref, kind_ref, count_ref, group_ref, factor_ref, own_ref, twin_ref, theta_ref, phi_ref, phase_ref, o_ref, far_ref, far_count_ref, theta_out, phi_out, cos_ref, sin_ref, list_ref, near_count_ref, all_ref):
    members = own_ref.shape[0]
    targets, slots = source_ref.shape
    waves, directions = o_ref.shape[2:]
    wide = 2 * members
    group = group_ref[0]
    far_group = group + 2 * (group & 1) - 1

    def sort_target(t, carry):
        count = count_ref[t]

        def sort_slot(k, counts):
            near, far = counts
            source = source_ref[t, k]
            place = lax.div(source, members)
            at = source - place * members
            entry = kind_ref[t, k] * wide + at
            list_ref[t, near] = entry + jnp.where(place == group, 0, members)
            far_ref[t, far] = entry
            is_far = jnp.where(place == far_group, 1, 0)
            return near + 1 - is_far, far + is_far

        near, far = lax.fori_loop(0, count, sort_slot, (0, 0))
        near_count_ref[t] = near
        far_count_ref[t] = far
        return carry

    lax.fori_loop(0, targets, sort_target, 0)

    all_ref[pl.ds(0, members)] = own_ref[...]
    all_ref[pl.ds(members, members)] = twin_ref[...]

    def target_body(t, carry):
        zero = jnp.zeros((waves, directions), f32)
        real, imag = add_slots(lambda k: list_ref[t, k], near_count_ref[t], factor_ref, all_ref, (zero, zero), wide)
        o_ref[t, 0] = real
        o_ref[t, 1] = imag
        return carry

    lax.fori_loop(0, targets, target_body, 0)

    coarse_t, fine_t = theta_ref.shape
    coarse_p, fine_p = phi_ref.shape
    span = BLOCK // fine_p
    spread_t = picker((fine_t, fine_t * SUB), lambda r, c: r == c // SUB)
    big = (coarse_t * SUB, fine_t * SUB)
    keep = iota(big, 0) % SUB == iota(big, 1) % SUB
    kh, kl = [theta_rows(part, coarse_t, lambda p: mm(p, spread_t), keep) for part in split(theta_ref[...])]
    theta_out[...] = jnp.concatenate([kh, kh, kl], axis=1)
    narrow = span * coarse_p
    spread_p = picker((coarse_p, narrow), lambda r, c: r == c % coarse_p)
    shape = (BLOCK, narrow)
    diag = iota(shape, 0) // fine_p == iota(shape, 1) // coarse_p

    def phi_block(part):
        rows = jnp.concatenate([mm_tn(part, spread_p)] * span, axis=0)
        return jnp.where(diag, rows, 0.0).astype(bf16)

    phi_out[...] = jnp.concatenate([phi_block(part) for part in split(phi_ref[...])], axis=1)
    sine, cosine = sincos(phase_ref[...])
    cos_ref[...] = cosine
    sin_ref[...] = sine


def far_kernel(far_ref, far_count_ref, factor_ref, data_ref, near_ref, o_ref):
    targets = near_ref.shape[0]
    wide = 2 * data_ref.shape[0]

    def target_body(t, carry):
        acc = near_ref[t, 0], near_ref[t, 1]
        real, imag = add_slots(lambda k: far_ref[t, k], far_count_ref[t], factor_ref, data_ref, acc, wide)
        o_ref[t, 0] = real
        o_ref[t, 1] = imag
        return carry

    lax.fori_loop(0, targets, target_body, 0)


def disaggregate_kernel(r_ref, weights_ref, phi_weights_ref, cos_ref, sin_ref, o_ref, o_buf, mid_ref, sems):
    fine_t, groups, _, rows = mid_ref.shape
    narrow = phi_weights_ref.shape[1] // 2
    span = narrow // (groups * SUB)
    per_member = r_ref.shape[3]
    columns = rows // 2
    coarse_t = o_ref.shape[1]
    unit = min(BLOCK, per_member)
    many = BLOCK // unit

    def body(pair, carry):
        for i in range(PAIR):
            step = pair * PAIR + i
            parts = [[], []]
            for piece in range(many):
                at = step * BLOCK + piece * unit
                member = lax.div(at, per_member)
                offset = pl.multiple_of(at - member * per_member, unit)
                for part in range(2):
                    parts[part].append(r_ref[member, part, :, pl.ds(offset, unit)])
            real, imag = [jnp.concatenate(p, axis=1)[None] for p in parts]
            lanes = pl.ds(pl.multiple_of(step * BLOCK, BLOCK), BLOCK)
            c = cos_ref[:, lanes][:, None, :]
            s = sin_ref[:, lanes][:, None, :]
            local = jnp.concatenate(
                [
                    (real * c + imag * s).reshape(columns, BLOCK),
                    (imag * c - real * s).reshape(columns, BLOCK),
                ],
                axis=0,
            )
            hi, lo = split(local)
            y = mm(jnp.concatenate([hi, lo], axis=0), phi_weights_ref[...])
            folded = y[:rows, :narrow] + (y[rows:, :narrow] + y[:rows, narrow:])
            mid_ref[pl.ds(step * span, span)] = folded.T.reshape(span, groups, SUB, rows)
        return carry

    lax.fori_loop(0, fine_t // span // PAIR, body, 0)

    copies = []
    for g in range(groups):
        hi, lo = split(mid_ref[:, g].reshape(fine_t * SUB, rows))
        coarse = mm(weights_ref[...], jnp.concatenate([hi, lo, hi], axis=0))
        for part in range(2):
            o_buf[part, :, g] = coarse[:, part * columns : (part + 1) * columns].reshape(coarse_t, SUB, columns)
        copies.append(pltpu.make_async_copy(o_buf.at[:, :, g], o_ref.at[:, :, g], sems.at[g]))
        copies[-1].start()
    for copy in copies:
        copy.wait()


def vmem():
    return pl.BlockSpec(memory_space=pltpu.VMEM)


def smem():
    return pl.BlockSpec(memory_space=pltpu.SMEM)


def hbm():
    return pl.BlockSpec(memory_space=pltpu.HBM)


def per_device(
    child_field,
    theta_interp,
    phi_interp,
    child_phase,
    translation,
    inter_source,
    inter_kind,
    inter_count,
    *,
    interpret=False,
):
    def call(*args, limit=VMEM_LIMIT, **kw):
        params = pltpu.CompilerParams(vmem_limit_bytes=limit)
        return pl.pallas_call(*args, interpret=interpret, compiler_params=params, **kw)

    shape = jax.ShapeDtypeStruct
    dma = pltpu.SemaphoreType.DMA
    branch, fine = child_phase.shape
    columns = child_field.shape[2]
    waves = columns // branch
    fine_t, coarse_t = theta_interp.shape
    fine_p, coarse_p = phi_interp.shape
    groups = coarse_p // SUB
    narrow = BLOCK // fine_p * coarse_p
    members = lax.axis_size("mem")
    grp_count = lax.axis_size("grp")
    per_member = fine // members
    targets, slots = inter_source.shape
    theta_t = theta_interp.T
    phi_t = phi_interp.T
    factors = jnp.transpose(translation, (1, 0, 2))
    block = (members, 2, waves, per_member)
    field = child_field.reshape(2, coarse_t, groups, SUB, columns)
    mid = pltpu.VMEM((fine_t, groups, SUB, 2 * columns), f32)
    phases = (branch, fine)

    summed = call(
        aggregate_kernel,
        out_shape=shape(block, f32),
        in_specs=[hbm()] * 4,
        out_specs=hbm(),
        scratch_shapes=[
            pltpu.VMEM(field.shape, f32),
            pltpu.VMEM(theta_t.shape, f32),
            pltpu.VMEM(phi_t.shape, f32),
            pltpu.VMEM(phases, f32),
            pltpu.VMEM(block, f32),
            mid,
            pltpu.VMEM(phases, f32),
            pltpu.VMEM(phases, f32),
            dma((groups,)),
            dma((3,)),
            dma((members,)),
        ],
        name="aggregate",
        limit=VMEM_WHOLE,
    )(field, theta_t, phi_t, child_phase)

    def exchange(x):
        return lax.all_to_all(x, "mem", split_axis=0, concat_axis=0, tiled=True)

    def swap(x, first):
        pairs = [(i, i + 1) for i in range(first, grp_count - 1, 2)]
        return lax.ppermute(x, "grp", pairs + [(j, i) for i, j in pairs])

    own = exchange(summed)
    far = swap(own, 1)
    twin = swap(own, 0)
    group = lax.axis_index("grp").astype(jnp.int32).reshape(1)
    near_cost = pl.CostEstimate(flops=COST, transcendentals=0, bytes_accessed=1 << 20)
    partial, far_list, far_count, theta_w, phi_w, cosine, sine = call(
        near_kernel,
        out_shape=(
            shape(block, f32),
            shape((targets, slots + 1), jnp.int32),
            shape((targets,), jnp.int32),
            shape((coarse_t * SUB, 3 * fine_t * SUB), bf16),
            shape((BLOCK, 2 * narrow), bf16),
            shape(phases, f32),
            shape(phases, f32),
        ),
        in_specs=[smem()] * 4 + [vmem()] * 6,
        out_specs=(vmem(), smem(), smem(), vmem(), vmem(), vmem(), vmem()),
        scratch_shapes=[
            pltpu.SMEM((targets, slots + 1), jnp.int32),
            pltpu.SMEM((targets,), jnp.int32),
            pltpu.VMEM((2 * members,) + block[1:], f32),
        ],
        name="near",
        cost_estimate=near_cost,
    )(inter_source, inter_kind, inter_count, group, factors, own, twin, theta_t, phi_t, child_phase)

    incoming = call(
        far_kernel,
        out_shape=shape(block, f32),
        in_specs=[smem()] * 2 + [vmem()] * 3,
        out_specs=vmem(),
        name="far",
    )(far_list, far_count, factors, far, partial)

    out = call(
        disaggregate_kernel,
        out_shape=shape(field.shape, f32),
        in_specs=[vmem()] * 5,
        out_specs=hbm(),
        scratch_shapes=[pltpu.VMEM(field.shape, f32), mid, dma((groups,))],
        name="disaggregate",
    )(exchange(incoming), theta_w, phi_w, cosine, sine)
    return out.reshape(child_field.shape)


def solution(mesh):
    return jax.shard_map(
        per_device,
        mesh=mesh,
        in_specs=(
            P(None, None, ("grp", "mem")),
            P(),
            P(),
            P(),
            P(None, None, "mem"),
            P("grp", None),
            P("grp", None),
            P("grp"),
        ),
        out_specs=P(None, None, ("grp", "mem")),
        check_vma=False,
    )
```

time: 70.1 us -> 61.3 us (0.87)
  Pallas kernels: 21.6 us -> 18.3 us
  waiting for transfers between devices: 6.1 us -> 3.25 us
  starting transfers between devices: 6.71 us -> 4.8 us
  local copies, waits for them, and re-layouts: 0.8 us -> 0.03 us
    pallas_call x3 -> x4, Pallas kernels: 21.6 us -> 18.3 us  [the longest x1 7.65 us: per_device(): call(aggregate_kernel, out_shape=shape(block, f32), in_specs=[hbm()] * 4,...]
    ppermute x2, waiting for transfers between devices: 6.1 us -> 3.25 us  [swap(): return lax.ppermute(x, 'grp', pairs + [(j, i) for i, j in pairs])]
    ppermute x2, starting transfers between devices: 6.71 us -> 4.8 us  [swap(): return lax.ppermute(x, 'grp', pairs + [(j, i) for i, j in pairs])]
    unnamed x6 -> x14, local copies, waits for them, and re-layouts: 0.8 us -> 0.03 us
  transfers between devices with their start and end apart: 2 -> 2, of which waited for: 2 -> 1; matrix products, arithmetic and copies ran while one was open for 0% -> 0% of each run, Pallas kernels for 0% -> 7%
where the time goes in v2:
time: 61.3 us; the launch traced here: 61.1 us
  blocking collectives  34.6 us (56%)
  Pallas kernels  18.3 us (30%)
  starting transfers between devices  4.8 us (8%)
  waiting for transfers between devices  3.25 us (5%)
    all_to_all x2, blocking collectives, exchange(): return lax.all_to_all(x, 'mem', split_axis=0, concat_axis=0, tiled=True)  34.6 us
    pallas_call x1, Pallas kernels, per_device(): call(aggregate_kernel, out_shape=shape(block, f32), in_specs=[hbm()] * 4,...  7.65 us
    pallas_call x1, Pallas kernels, per_device(): call(disaggregate_kernel, out_shape=shape(field.shape, f32), in_specs=[vm...  5.15 us
    ppermute x2, starting transfers between devices, swap(): return lax.ppermute(x, 'grp', pairs + [(j, i) for i, j in pairs])  4.8 us
    pallas_call x1, Pallas kernels, per_device(): call(near_kernel, out_shape=(shape(block, f32), shape((targets, slots + 1...  4.13 us
    ppermute x2, waiting for transfers between devices, swap(): return lax.ppermute(x, 'grp', pairs + [(j, i) for i, j in pairs])  3.25 us
    pallas_call x1, Pallas kernels, per_device(): call(far_kernel, out_shape=shape(block, f32), in_specs=[smem()] * 2 + [vm...  1.33 us
  transfers between devices with their start and end apart: 2, of which 1 were waited for; matrix products, arithmetic and copies ran while one was open for 0% of the time, Pallas kernels for 7%

profile of v2, /device:TPU:1, one launch (start us, length us, event | category | flops | bytes accessed | tf_op | source)
XLA Modules:
  0.0 61.1 jit_solution(1726164352480030012)
XLA Ops:
  0.0 0.0 copy-start
  0.0 0.0 copy-start.1
  0.0 0.0 copy-start.2
  0.0 0.0 copy-start.3
  0.0 0.0 copy-start.4
  0.0 0.0 copy-start.5
  0.0 0.0 copy-start.6
  0.0 7.7 %aggregate.1 = f32[8,2,16,512]{3,2,1,0:T(8,128)} custom-call(f32[2,32,4,8,128]{4,3,2,1,0:T(8,128)} %bitcast.12, f32[32,64]{1,0:T(8,128)} %bitcast.8, f32[32,64]{1,0:T(8,128)} %bitcast.10, f32[8,4096]{1,0:T(8,128)} %phase_ref.3), custom_call_target="tpu_custom_call" | custom-call | tf_op jit(solution)/shard_map/aggregate/pallas_call | solution.py:344
  7.7 20.1 %all_to_all.10.own_ref = f32[8,2,16,512]{3,2,1,0:T(8,128)S(1)} all-to-all(f32[8,2,16,512]{3,2,1,0:T(8,128)} %aggregate.1), channel_id=1, replica_groups=mesh['grp'=4,'mem'=8] {'mem'}, dimensions={0} | all-to-all | bytes 1048576 | tf_op jit(solution)/shard_map/all_to_all | solution.py:367
  27.8 1.8 %collective-permute-start = (f32[8,2,16,512]{3,2,1,0:T(8,128)S(1)}, f32[8,2,16,512]{3,2,1,0:T(8,128)S(1)}, u32[]{:S(2)}, u32[]{:S(2)}) collective-permute-start(f32[8,2,16,512]{3,2,1,0:T(8,128)S(1)} %all_to_all.10.own_ref), channel_id=1, source_target_pairs={{0,8},{16,24},{8,0},{24,16},{1,9},{17,25},{9,1},{25,17},{2,10},{18... | collective-permute-start | bytes 1572872 | tf_op jit(solution)/shard_map/ppermute | solution.py:371
  29.6 3.0 %collective-permute-start.1 = (f32[8,2,16,512]{3,2,1,0:T(8,128)S(1)}, f32[8,2,16,512]{3,2,1,0:T(8,128)S(1)}, u32[]{:S(2)}, u32[]{:S(2)}) collective-permute-start(f32[8,2,16,512]{3,2,1,0:T(8,128)S(1)} %all_to_all.10.own_ref), channel_id=1, source_target_pairs={{8,16},{16,8},{9,17},{17,9},{10,18},{18,10},{11,19},{19,11},{12,20... | collective-permute-start | bytes 1572872 | tf_op jit(solution)/shard_map/ppermute | solution.py:371
  32.6 0.0 collective-permute-done.twin_ref
  32.6 0.0 copy-done
  32.6 0.0 copy-done.1
  32.6 0.0 copy-done.2
  32.6 0.0 copy-done.3
  32.6 0.0 copy-done.4
  32.6 0.0 copy-done.5
  32.7 0.0 copy-done.6
  32.7 4.1 %near.1 = (f32[8,2,16,512]{3,2,1,0:T(8,128)S(1)}, s32[8,25]{1,0:T(8,128)S(1)}, s32[8]{0:T(128)S(1)}, bf16[256,1536]{1,0:T(8,128)(2,1)S(1)}, bf16[256,256]{1,0:T(...) custom-call(s32[8,24]{1,0:T(8,128)S(1)} %copy-done.4, s32[8,24]{1,0:T(8,128)S(1)} %copy-done.5, ...), custom_call_target="tpu_custom_call" | custom-call | flops 50000000 | bytes 1048576 | tf_op jit(solution)/shard_map/near/pallas_call | solution.py:378
  36.8 3.3 %collective-permute-done.1.data_ref = f32[8,2,16,512]{3,2,1,0:T(8,128)S(1)} collective-permute-done((f32[8,2,16,512]{3,2,1,0:T(8,128)S(1)}, f32[8,2,16,512]{3,2,1,0:T(8,128)S(1)}, u32[]{:S(2)}, u32[]{:S(2)}) %collective-permute-start.1) | collective-permute-done | bytes 524320 | tf_op jit(solution)/shard_map/ppermute | solution.py:371
  40.1 1.3 %far.1 = f32[8,2,16,512]{3,2,1,0:T(8,128)S(1)} custom-call(s32[8,25]{1,0:T(8,128)S(1)} %get-tuple-element.12.far_ref, s32[8]{0:T(128)S(1)} %get-tuple-element.13.far_count_ref, f32[316,2,512]{2,1,0:T(2,128)S(1)} %bitcast.7, f32[8,2,16,512]{3,2,1,0:T(8,128)S(1)} %collective-permute-done.1.data_ref, f32[8,2,16,512]{3,2,1,0:T(8,128)S(1)} %get-tuple-element.14.near_ref), custom_call_target="tpu_custom_call" | custom-call | tf_op jit(solution)/shard_map/far/pallas_call | solution.py:400
  41.4 14.5 %all_to_all.11.r_ref = f32[8,2,16,512]{3,2,1,0:T(8,128)S(1)} all-to-all(f32[8,2,16,512]{3,2,1,0:T(8,128)S(1)} %far.1), channel_id=1, replica_groups=mesh['grp'=4,'mem'=8] {'mem'}, dimensions={0} | all-to-all | bytes 1048576 | tf_op jit(solution)/shard_map/all_to_all | solution.py:367
  55.9 5.2 %disaggregate.1 = f32[2,32,4,8,128]{4,3,2,1,0:T(8,128)} custom-call(f32[8,2,16,512]{3,2,1,0:T(8,128)S(1)} %all_to_all.11.r_ref, bf16[256,1536]{1,0:T(8,128)(2,1)S(1)} %get-tuple-element.15.weights_ref, bf16[256,256]{1,0:T(8,128)(2,1)S(1)} %get-tuple-element.16.phi_weights_ref, f32[8,4096]{1,0:T(8,128)S(1)} %get-tuple-element.17.cos_ref, ...), custom_call_target="tpu_custom_call" | custom-call | tf_op jit(solution)/shard_map/disaggregate/pallas_call | solution.py:408
Async XLA Ops:
  0.0 32.6 %copy-start = (f32[2,316,512]{2,0,1:T(2,128)S(1)}, f32[2,316,512]{2,0,1:T(2,128)}, u32[]{:S(2)}) copy-start(f32[2,316,512]{2,0,1:T(2,128)} %param.12) | copy-start | bytes 3883012
  0.0 32.6 %copy-start.1 = (f32[8,4096]{1,0:T(8,128)S(1)}, f32[8,4096]{1,0:T(8,128)}, u32[]{:S(2)}) copy-start(f32[8,4096]{1,0:T(8,128)} %phase_ref.3) | copy-start | bytes 393220
  0.0 32.6 %copy-start.2 = (f32[64,32]{0,1:T(8,128)S(1)}, f32[64,32]{0,1:T(8,128)}, u32[]{:S(2)}) copy-start(f32[64,32]{0,1:T(8,128)} %param.9) | copy-start | bytes 24580
  0.0 32.6 %copy-start.3 = (f32[64,32]{0,1:T(8,128)S(1)}, f32[64,32]{0,1:T(8,128)}, u32[]{:S(2)}) copy-start(f32[64,32]{0,1:T(8,128)} %param.10) | copy-start | bytes 24580
  0.0 32.6 %copy-start.4 = (s32[8,24]{1,0:T(8,128)S(1)}, s32[8,24]{1,0:T(8,128)}, u32[]{:S(2)}) copy-start(s32[8,24]{1,0:T(8,128)} %source_ref.1) | copy-start | bytes 2308
  0.0 32.6 %copy-start.5 = (s32[8,24]{1,0:T(8,128)S(1)}, s32[8,24]{1,0:T(8,128)}, u32[]{:S(2)}) copy-start(s32[8,24]{1,0:T(8,128)} %kind_ref.1) | copy-start | bytes 2308
  0.0 32.6 %copy-start.6 = (s32[8]{0:T(128)S(1)}, s32[8]{0:T(128)}, u32[]{:S(2)}) copy-start(s32[8]{0:T(128)} %count_ref.1) | copy-start | bytes 100
  27.8 4.8 %collective-permute-start = (f32[8,2,16,512]{3,2,1,0:T(8,128)S(1)}, f32[8,2,16,512]{3,2,1,0:T(8,128)S(1)}, u32[]{:S(2)}, u32[]{:S(2)}) collective-permute-start(f32[8,2,16,512]{3,2,1,0:T(8,128)S(1)} %all_to_all.10.own_ref), channel_id=1, source_target_pairs={{0,8},{16,24},{8,0},{24,16},{1,9},{17,25},{9,1},{25,17},{2,10},{18... | collective-permute-start | bytes 1572872 | tf_op jit(solution)/shard_map/ppermute | solution.py:371
  29.6 10.5 %collective-permute-start.1 = (f32[8,2,16,512]{3,2,1,0:T(8,128)S(1)}, f32[8,2,16,512]{3,2,1,0:T(8,128)S(1)}, u32[]{:S(2)}, u32[]{:S(2)}) collective-permute-start(f32[8,2,16,512]{3,2,1,0:T(8,128)S(1)} %all_to_all.10.own_ref), channel_id=1, source_target_pairs={{8,16},{16,8},{9,17},{17,9},{10,18},{18,10},{11,19},{19,11},{12,20... | collective-permute-start | bytes 1572872 | tf_op jit(solution)/shard_map/ppermute | solution.py:371

commit v3 on v2

--- a/solution.py
+++ b/solution.py
@@ -10,7 +10,7 @@
 SUB = 8
 BLOCK = 256
 UNROLL = 4
-PAIR = 2
+PAIR = 16
 COST = 50_000_000
 VMEM_LIMIT = 20 << 20
 VMEM_WHOLE = 60 * 1024 * 1024
@@ -58,7 +58,7 @@
     return jnp.where(keep, rows, 0.0).astype(bf16)
 
 
-def aggregate_kernel(x_ref, theta_ref, phi_ref, phase_ref, o_ref, x_buf, theta_buf, phi_buf, phase_buf, o_buf, mid_ref, cos_ref, sin_ref, x_sems, sems, o_sems):
+def aggregate_kernel(x_ref, theta_ref, phi_ref, phase_ref, o_ref, x_buf, theta_buf, phi_buf, phase_buf, mid_ref, cos_ref, sin_ref, x_sems, sems):
     coarse_t, fine_t = theta_ref.shape
     coarse_p, fine_p = phi_ref.shape
     groups = coarse_p // SUB
@@ -108,9 +108,6 @@
     unit = min(BLOCK, per_member)
     batch = max(per_member, PAIR * BLOCK)
     many = batch // per_member
-
-    def out_copy(member):
-        return pltpu.make_async_copy(o_buf.at[member], o_ref.at[member], o_sems.at[member])
 
     def body(step, carry):
         for i in range(batch // BLOCK):
@@ -128,18 +125,10 @@
                 member = step * many + at // per_member
                 there = pl.ds(at % per_member, unit)
                 for part in range(2):
-                    o_buf[member, part, :, there] = outs[part][:, piece * unit : (piece + 1) * unit]
-        for j in range(many):
-            out_copy(step * many + j).start()
+                    o_ref[member, part, :, there] = outs[part][:, piece * unit : (piece + 1) * unit]
         return carry
 
     lax.fori_loop(0, fine // batch, body, 0)
-
-    def drain(member, carry):
-        out_copy(member).wait()
-        return carry
-
-    lax.fori_loop(0, members, drain, 0)
 
 
 def add_slots(entry_of, count, factor_ref, data_ref, acc, wide):
@@ -345,23 +334,21 @@
         aggregate_kernel,
         out_shape=shape(block, f32),
         in_specs=[hbm()] * 4,
-        out_specs=hbm(),
+        out_specs=vmem(),
         scratch_shapes=[
             pltpu.VMEM(field.shape, f32),
             pltpu.VMEM(theta_t.shape, f32),
             pltpu.VMEM(phi_t.shape, f32),
             pltpu.VMEM(phases, f32),
-            pltpu.VMEM(block, f32),
             mid,
             pltpu.VMEM(phases, f32),
             pltpu.VMEM(phases, f32),
             dma((groups,)),
             dma((3,)),
-            dma((members,)),
         ],
         name="aggregate",
-        limit=VMEM_WHOLE,
-    )(field, theta_t, phi_t, child_phase)
+
+    )(*[pltpu.with_memory_space_constraint(v, pltpu.HBM) for v in (field, theta_t, phi_t, child_phase)])
 
     def exchange(x):
         return lax.all_to_all(x, "mem", split_axis=0, concat_axis=0, tiled=True)

time: 61.3 us -> 57 us (0.930)
  Pallas kernels: 18.3 us -> 14.2 us
    pallas_call x1, Pallas kernels: 7.65 us -> 5.29 us  [per_device(): call(aggregate_kernel, out_shape=shape(block, f32), in_specs=[hbm()] * 4,...]
    pallas_call x1, Pallas kernels: 5.15 us -> 3.46 us  [per_device(): call(disaggregate_kernel, out_shape=shape(field.shape, f32), in_specs=[vm...]
where the time goes in v3:
time: 57 us; the launch traced here: 56.8 us
  blocking collectives  34.4 us (60%)
  Pallas kernels  14.2 us (25%)
  starting transfers between devices  4.79 us (8%)
  waiting for transfers between devices  3.26 us (6%)
    all_to_all x2, blocking collectives, exchange(): return lax.all_to_all(x, 'mem', split_axis=0, concat_axis=0, tiled=True)  34.4 us
    pallas_call x1, Pallas kernels, per_device(): call(aggregate_kernel, out_shape=shape(block, f32), in_specs=[hbm()] * 4,...  5.29 us
    ppermute x2, starting transfers between devices, swap(): return lax.ppermute(x, 'grp', pairs + [(j, i) for i, j in pairs])  4.79 us
    pallas_call x1, Pallas kernels, per_device(): call(near_kernel, out_shape=(shape(block, f32), shape((targets, slots + 1...  4.13 us
    pallas_call x1, Pallas kernels, per_device(): call(disaggregate_kernel, out_shape=shape(field.shape, f32), in_specs=[vm...  3.46 us
    ppermute x2, waiting for transfers between devices, swap(): return lax.ppermute(x, 'grp', pairs + [(j, i) for i, j in pairs])  3.26 us
    pallas_call x1, Pallas kernels, per_device(): call(far_kernel, out_shape=shape(block, f32), in_specs=[smem()] * 2 + [vm...  1.33 us
  transfers between devices with their start and end apart: 2, of which 1 were waited for; matrix products, arithmetic and copies ran while one was open for 0% of the time, Pallas kernels for 7%

profile of v3, /device:TPU:1, one launch (start us, length us, event | category | flops | bytes accessed | tf_op | source)
XLA Modules:
  0.0 56.8 jit_solution(5618665613201740979)
XLA Ops:
  0.0 0.0 copy-start
  0.0 0.0 copy-start.1
  0.0 0.0 copy-start.2
  0.0 0.0 copy-start.3
  0.0 0.0 copy-start.4
  0.0 0.0 copy-start.5
  0.0 0.0 copy-start.6
  0.0 5.3 %aggregate.1 = f32[8,2,16,512]{3,2,1,0:T(8,128)S(1)} custom-call(f32[2,32,4,8,128]{4,3,2,1,0:T(8,128)} %bitcast.12, f32[32,64]{1,0:T(8,128)} %bitcast.8, f32[32,64]{1,0:T(8,128)} %bitcast.10, f32[8,4096]{1,0:T(8,128)} %phase_ref.3), custom_call_target="tpu_custom_call" | custom-call | tf_op jit(solution)/shard_map/aggregate/pallas_call | solution.py:333
  5.3 19.9 %all_to_all.10.own_ref = f32[8,2,16,512]{3,2,1,0:T(8,128)S(1)} all-to-all(f32[8,2,16,512]{3,2,1,0:T(8,128)S(1)} %aggregate.1), channel_id=1, replica_groups=mesh['grp'=4,'mem'=8] {'mem'}, dimensions={0} | all-to-all | bytes 1048576 | tf_op jit(solution)/shard_map/all_to_all | solution.py:354
  25.2 1.8 %collective-permute-start = (f32[8,2,16,512]{3,2,1,0:T(8,128)S(1)}, f32[8,2,16,512]{3,2,1,0:T(8,128)S(1)}, u32[]{:S(2)}, u32[]{:S(2)}) collective-permute-start(f32[8,2,16,512]{3,2,1,0:T(8,128)S(1)} %all_to_all.10.own_ref), channel_id=1, source_target_pairs={{0,8},{16,24},{8,0},{24,16},{1,9},{17,25},{9,1},{25,17},{2,10},{18... | collective-permute-start | bytes 1572872 | tf_op jit(solution)/shard_map/ppermute | solution.py:358
  27.0 3.0 %collective-permute-start.1 = (f32[8,2,16,512]{3,2,1,0:T(8,128)S(1)}, f32[8,2,16,512]{3,2,1,0:T(8,128)S(1)}, u32[]{:S(2)}, u32[]{:S(2)}) collective-permute-start(f32[8,2,16,512]{3,2,1,0:T(8,128)S(1)} %all_to_all.10.own_ref), channel_id=1, source_target_pairs={{8,16},{16,8},{9,17},{17,9},{10,18},{18,10},{11,19},{19,11},{12,20... | collective-permute-start | bytes 1572872 | tf_op jit(solution)/shard_map/ppermute | solution.py:358
  30.0 0.0 collective-permute-done.twin_ref
  30.0 0.0 copy-done
  30.0 0.0 copy-done.1
  30.0 0.0 copy-done.2
  30.1 0.0 copy-done.3
  30.1 0.0 copy-done.4
  30.1 0.0 copy-done.5
  30.1 0.0 copy-done.6
  30.1 4.1 %near.1 = (f32[8,2,16,512]{3,2,1,0:T(8,128)S(1)}, s32[8,25]{1,0:T(8,128)S(1)}, s32[8]{0:T(128)S(1)}, bf16[256,1536]{1,0:T(8,128)(2,1)S(1)}, bf16[256,256]{1,0:T(...) custom-call(s32[8,24]{1,0:T(8,128)S(1)} %copy-done.4, s32[8,24]{1,0:T(8,128)S(1)} %copy-done.5, ...), custom_call_target="tpu_custom_call" | custom-call | flops 50000000 | bytes 1048576 | tf_op jit(solution)/shard_map/near/pallas_call | solution.py:365
  34.2 3.3 %collective-permute-done.1.data_ref = f32[8,2,16,512]{3,2,1,0:T(8,128)S(1)} collective-permute-done((f32[8,2,16,512]{3,2,1,0:T(8,128)S(1)}, f32[8,2,16,512]{3,2,1,0:T(8,128)S(1)}, u32[]{:S(2)}, u32[]{:S(2)}) %collective-permute-start.1) | collective-permute-done | bytes 524320 | tf_op jit(solution)/shard_map/ppermute | solution.py:358
  37.5 1.3 %far.1 = f32[8,2,16,512]{3,2,1,0:T(8,128)S(1)} custom-call(s32[8,25]{1,0:T(8,128)S(1)} %get-tuple-element.12.far_ref, s32[8]{0:T(128)S(1)} %get-tuple-element.13.far_count_ref, f32[316,2,512]{2,1,0:T(2,128)S(1)} %bitcast.7, f32[8,2,16,512]{3,2,1,0:T(8,128)S(1)} %collective-permute-done.1.data_ref, f32[8,2,16,512]{3,2,1,0:T(8,128)S(1)} %get-tuple-element.14.near_ref), custom_call_target="tpu_custom_call" | custom-call | tf_op jit(solution)/shard_map/far/pallas_call | solution.py:387
  38.8 14.5 %all_to_all.11.r_ref = f32[8,2,16,512]{3,2,1,0:T(8,128)S(1)} all-to-all(f32[8,2,16,512]{3,2,1,0:T(8,128)S(1)} %far.1), channel_id=1, replica_groups=mesh['grp'=4,'mem'=8] {'mem'}, dimensions={0} | all-to-all | bytes 1048576 | tf_op jit(solution)/shard_map/all_to_all | solution.py:354
  53.4 3.5 %disaggregate.1 = f32[2,32,4,8,128]{4,3,2,1,0:T(8,128)} custom-call(f32[8,2,16,512]{3,2,1,0:T(8,128)S(1)} %all_to_all.11.r_ref, bf16[256,1536]{1,0:T(8,128)(2,1)S(1)} %get-tuple-element.15.weights_ref, bf16[256,256]{1,0:T(8,128)(2,1)S(1)} %get-tuple-element.16.phi_weights_ref, f32[8,4096]{1,0:T(8,128)S(1)} %get-tuple-element.17.cos_ref, ...), custom_call_target="tpu_custom_call" | custom-call | tf_op jit(solution)/shard_map/disaggregate/pallas_call | solution.py:395
Async XLA Ops:
  0.0 30.0 %copy-start = (f32[2,316,512]{2,0,1:T(2,128)S(1)}, f32[2,316,512]{2,0,1:T(2,128)}, u32[]{:S(2)}) copy-start(f32[2,316,512]{2,0,1:T(2,128)} %param.12) | copy-start | bytes 3883012
  0.0 30.0 %copy-start.1 = (f32[8,4096]{1,0:T(8,128)S(1)}, f32[8,4096]{1,0:T(8,128)}, u32[]{:S(2)}) copy-start(f32[8,4096]{1,0:T(8,128)} %phase_ref.3) | copy-start | bytes 393220
  0.0 30.0 %copy-start.2 = (f32[64,32]{0,1:T(8,128)S(1)}, f32[64,32]{0,1:T(8,128)}, u32[]{:S(2)}) copy-start(f32[64,32]{0,1:T(8,128)} %param.9) | copy-start | bytes 24580
  0.0 30.0 %copy-start.3 = (f32[64,32]{0,1:T(8,128)S(1)}, f32[64,32]{0,1:T(8,128)}, u32[]{:S(2)}) copy-start(f32[64,32]{0,1:T(8,128)} %param.10) | copy-start | bytes 24580
  0.0 30.0 %copy-start.4 = (s32[8,24]{1,0:T(8,128)S(1)}, s32[8,24]{1,0:T(8,128)}, u32[]{:S(2)}) copy-start(s32[8,24]{1,0:T(8,128)} %source_ref.1) | copy-start | bytes 2308
  0.0 30.0 %copy-start.5 = (s32[8,24]{1,0:T(8,128)S(1)}, s32[8,24]{1,0:T(8,128)}, u32[]{:S(2)}) copy-start(s32[8,24]{1,0:T(8,128)} %kind_ref.1) | copy-start | bytes 2308
  0.0 30.0 %copy-start.6 = (s32[8]{0:T(128)S(1)}, s32[8]{0:T(128)}, u32[]{:S(2)}) copy-start(s32[8]{0:T(128)} %count_ref.1) | copy-start | bytes 100
  25.2 4.8 %collective-permute-start = (f32[8,2,16,512]{3,2,1,0:T(8,128)S(1)}, f32[8,2,16,512]{3,2,1,0:T(8,128)S(1)}, u32[]{:S(2)}, u32[]{:S(2)}) collective-permute-start(f32[8,2,16,512]{3,2,1,0:T(8,128)S(1)} %all_to_all.10.own_ref), channel_id=1, source_target_pairs={{0,8},{16,24},{8,0},{24,16},{1,9},{17,25},{9,1},{25,17},{2,10},{18... | collective-permute-start | bytes 1572872 | tf_op jit(solution)/shard_map/ppermute | solution.py:358
  27.0 10.5 %collective-permute-start.1 = (f32[8,2,16,512]{3,2,1,0:T(8,128)S(1)}, f32[8,2,16,512]{3,2,1,0:T(8,128)S(1)}, u32[]{:S(2)}, u32[]{:S(2)}) collective-permute-start(f32[8,2,16,512]{3,2,1,0:T(8,128)S(1)} %all_to_all.10.own_ref), channel_id=1, source_target_pairs={{8,16},{16,8},{9,17},{17,9},{10,18},{18,10},{11,19},{19,11},{12,20... | collective-permute-start | bytes 1572872 | tf_op jit(solution)/shard_map/ppermute | solution.py:358

commit v4 on v3

--- a/solution.py
+++ b/solution.py
@@ -20,6 +20,15 @@
     hi = x.astype(bf16)
     lo = (x - hi.astype(f32)).astype(bf16)
     return hi, lo
+
+
+def seat(member, members):
+    half = member // 2
+    return half + (member % 2) * (members - 1 - 2 * half)
+
+
+def seating(members):
+    return sorted(range(members), key=lambda m: seat(m, members))
 
 
 def mm(a, b):
@@ -58,7 +67,7 @@
     return jnp.where(keep, rows, 0.0).astype(bf16)
 
 
-def aggregate_kernel(x_ref, theta_ref, phi_ref, phase_ref, o_ref, x_buf, theta_buf, phi_buf, phase_buf, mid_ref, cos_ref, sin_ref, x_sems, sems):
+def aggregate_kernel(x_ref, theta_ref, phi_ref, phase_ref, o_ref, cos_ref, sin_ref, x_buf, theta_buf, phi_buf, phase_buf, mid_ref, x_sems, sems):
     coarse_t, fine_t = theta_ref.shape
     coarse_p, fine_p = phi_ref.shape
     groups = coarse_p // SUB
@@ -122,7 +131,7 @@
             outs = jnp.sum(real * c - imag * s, axis=0), jnp.sum(imag * c + real * s, axis=0)
             for piece in range(BLOCK // unit):
                 at = i * BLOCK + piece * unit
-                member = step * many + at // per_member
+                member = seat(step * many + at // per_member, members)
                 there = pl.ds(at % per_member, unit)
                 for part in range(2):
                     o_ref[member, part, :, there] = outs[part][:, piece * unit : (piece + 1) * unit]
@@ -152,7 +161,7 @@
     return lax.fori_loop(0, lax.div(count + (UNROLL - 1), UNROLL), slot_body, acc)
 
 
-def near_kernel(source_ref, kind_ref, count_ref, group_ref, factor_ref, own_ref, twin_ref, theta_ref, phi_ref, phase_ref, o_ref, far_ref, far_count_ref, theta_out, phi_out, cos_ref, sin_ref, list_ref, near_count_ref, all_ref):
+def near_kernel(source_ref, kind_ref, count_ref, group_ref, factor_ref, own_ref, twin_ref, theta_ref, phi_ref, o_ref, far_ref, far_count_ref, theta_out, phi_out, list_ref, near_count_ref, all_ref):
     members = own_ref.shape[0]
     targets, slots = source_ref.shape
     waves, directions = o_ref.shape[2:]
@@ -181,8 +190,9 @@
 
     lax.fori_loop(0, targets, sort_target, 0)
 
-    all_ref[pl.ds(0, members)] = own_ref[...]
-    all_ref[pl.ds(members, members)] = twin_ref[...]
+    for m in range(members):
+        all_ref[m] = own_ref[seat(m, members)]
+        all_ref[members + m] = twin_ref[seat(m, members)]
 
     def target_body(t, carry):
         zero = jnp.zeros((waves, directions), f32)
@@ -211,20 +221,20 @@
         return jnp.where(diag, rows, 0.0).astype(bf16)
 
     phi_out[...] = jnp.concatenate([phi_block(part) for part in split(phi_ref[...])], axis=1)
-    sine, cosine = sincos(phase_ref[...])
-    cos_ref[...] = cosine
-    sin_ref[...] = sine
-
-
-def far_kernel(far_ref, far_count_ref, factor_ref, data_ref, near_ref, o_ref):
+
+
+def far_kernel(far_ref, far_count_ref, factor_ref, far_data_ref, near_ref, o_ref, data_ref):
     targets = near_ref.shape[0]
-    wide = 2 * data_ref.shape[0]
+    members = data_ref.shape[0]
+    wide = 2 * members
+    for m in range(members):
+        data_ref[m] = far_data_ref[seat(m, members)]
 
     def target_body(t, carry):
         acc = near_ref[t, 0], near_ref[t, 1]
         real, imag = add_slots(lambda k: far_ref[t, k], far_count_ref[t], factor_ref, data_ref, acc, wide)
-        o_ref[t, 0] = real
-        o_ref[t, 1] = imag
+        o_ref[seat(t, targets), 0] = real
+        o_ref[seat(t, targets), 1] = imag
         return carry
 
     lax.fori_loop(0, targets, target_body, 0)
@@ -248,6 +258,7 @@
                 at = step * BLOCK + piece * unit
                 member = lax.div(at, per_member)
                 offset = pl.multiple_of(at - member * per_member, unit)
+                member = seat(member, r_ref.shape[0])
                 for part in range(2):
                     parts[part].append(r_ref[member, part, :, pl.ds(offset, unit)])
             real, imag = [jnp.concatenate(p, axis=1)[None] for p in parts]
@@ -330,19 +341,17 @@
     mid = pltpu.VMEM((fine_t, groups, SUB, 2 * columns), f32)
     phases = (branch, fine)
 
-    summed = call(
+    summed, cosine, sine = call(
         aggregate_kernel,
-        out_shape=shape(block, f32),
+        out_shape=(shape(block, f32), shape(phases, f32), shape(phases, f32)),
         in_specs=[hbm()] * 4,
-        out_specs=vmem(),
+        out_specs=(vmem(), vmem(), vmem()),
         scratch_shapes=[
             pltpu.VMEM(field.shape, f32),
             pltpu.VMEM(theta_t.shape, f32),
             pltpu.VMEM(phi_t.shape, f32),
             pltpu.VMEM(phases, f32),
             mid,
-            pltpu.VMEM(phases, f32),
-            pltpu.VMEM(phases, f32),
             dma((groups,)),
             dma((3,)),
         ],
@@ -351,7 +360,7 @@
     )(*[pltpu.with_memory_space_constraint(v, pltpu.HBM) for v in (field, theta_t, phi_t, child_phase)])
 
     def exchange(x):
-        return lax.all_to_all(x, "mem", split_axis=0, concat_axis=0, tiled=True)
+        return lax.all_to_all(x, "mem", split_axis=0, concat_axis=0, tiled=True, axis_index_groups=[seating(members)])
 
     def swap(x, first):
         pairs = [(i, i + 1) for i in range(first, grp_count - 1, 2)]
@@ -362,7 +371,7 @@
     twin = swap(own, 0)
     group = lax.axis_index("grp").astype(jnp.int32).reshape(1)
     near_cost = pl.CostEstimate(flops=COST, transcendentals=0, bytes_accessed=1 << 20)
-    partial, far_list, far_count, theta_w, phi_w, cosine, sine = call(
+    partial, far_list, far_count, theta_w, phi_w = call(
         near_kernel,
         out_shape=(
             shape(block, f32),
@@ -370,11 +379,9 @@
             shape((targets,), jnp.int32),
             shape((coarse_t * SUB, 3 * fine_t * SUB), bf16),
             shape((BLOCK, 2 * narrow), bf16),
-            shape(phases, f32),
-            shape(phases, f32),
         ),
-        in_specs=[smem()] * 4 + [vmem()] * 6,
-        out_specs=(vmem(), smem(), smem(), vmem(), vmem(), vmem(), vmem()),
+        in_specs=[smem()] * 4 + [vmem()] * 5,
+        out_specs=(vmem(), smem(), smem(), vmem(), vmem()),
         scratch_shapes=[
             pltpu.SMEM((targets, slots + 1), jnp.int32),
             pltpu.SMEM((targets,), jnp.int32),
@@ -382,13 +389,14 @@
         ],
         name="near",
         cost_estimate=near_cost,
-    )(inter_source, inter_kind, inter_count, group, factors, own, twin, theta_t, phi_t, child_phase)
+    )(inter_source, inter_kind, inter_count, group, factors, own, twin, theta_t, phi_t)
 
     incoming = call(
         far_kernel,
         out_shape=shape(block, f32),
         in_specs=[smem()] * 2 + [vmem()] * 3,
         out_specs=vmem(),
+        scratch_shapes=[pltpu.VMEM(block, f32)],
         name="far",
     )(far_list, far_count, factors, far, partial)
 

time: 57 us -> 56.7 us (level)
  blocking collectives: 34.4 us -> 32.8 us
  starting transfers between devices: 4.79 us -> 5.96 us
    all_to_all x2, blocking collectives: 34.4 us -> 32.8 us  [exchange(): lax.all_to_all(x, 'mem', split_axis=0, concat_axis=0, tiled=True, axis_in...]
    ppermute x2, starting transfers between devices: 4.79 us -> 5.96 us  [swap(): return lax.ppermute(x, 'grp', pairs + [(j, i) for i, j in pairs])]
where the time goes in v4:
time: 56.7 us; the launch traced here: 56.5 us
  blocking collectives  32.8 us (58%)
  Pallas kernels  14.3 us (25%)
  starting transfers between devices  5.96 us (11%)
  waiting for transfers between devices  3.27 us (6%)
    all_to_all x2, blocking collectives, exchange(): lax.all_to_all(x, 'mem', split_axis=0, concat_axis=0, tiled=True, axis_in...  32.8 us
    ppermute x2, starting transfers between devices, swap(): return lax.ppermute(x, 'grp', pairs + [(j, i) for i, j in pairs])  5.96 us
    pallas_call x1, Pallas kernels, per_device(): call(aggregate_kernel, out_shape=(shape(block, f32), shape(phases, f32),...  5.33 us
    pallas_call x1, Pallas kernels, per_device(): call(near_kernel, out_shape=(shape(block, f32), shape((targets, slots + 1...  4.13 us
    pallas_call x1, Pallas kernels, per_device(): call(disaggregate_kernel, out_shape=shape(field.shape, f32), in_specs=[vm...  3.45 us
    ppermute x2, waiting for transfers between devices, swap(): return lax.ppermute(x, 'grp', pairs + [(j, i) for i, j in pairs])  3.27 us
    pallas_call x1, Pallas kernels, per_device(): call(far_kernel, out_shape=shape(block, f32), in_specs=[smem()] * 2 + [vm...  1.42 us
  transfers between devices with their start and end apart: 2, of which 1 were waited for; matrix products, arithmetic and copies ran while one was open for 0% of the time, Pallas kernels for 7%

profile of v4, /device:TPU:1, one launch (start us, length us, event | category | flops | bytes accessed | tf_op | source)
XLA Modules:
  0.0 56.5 jit_solution(3643189369345432992)
XLA Ops:
  0.0 0.0 copy-start.1
  0.0 0.0 copy-start.2
  0.0 0.0 copy-start
  0.0 0.0 copy-start.3
  0.0 0.0 copy-start.4
  0.0 0.0 copy-start.5
  0.0 5.3 %aggregate.1 = (f32[8,2,16,512]{3,2,1,0:T(8,128)S(1)}, f32[8,4096]{1,0:T(8,128)S(1)}, f32[8,4096]{1,0:T(8,128)S(1)}) custom-call(f32[2,32,4,8,128]{4,3,2,1,0:T(8,128)} %bitcast.12, f32[32,64]{1,0:T(8,128)} %bitcast.8, f32[32,64]{1,0:T(8,128)} %bitcast.10, f32[8,4096]{1,0:T(8,128)} %phase_ref.1), custom_call_target="tpu_custom_call" | custom-call | tf_op jit(solution)/shard_map/aggregate/pallas_call | solution.py:344
  5.4 18.5 %all_to_all.10.own_ref = f32[8,2,16,512]{3,2,1,0:T(8,128)S(1)} all-to-all(f32[8,2,16,512]{3,2,1,0:T(8,128)S(1)} %get-tuple-element.13), channel_id=1, replica_groups={{0,2,4,6,7,5,3,1},{8,10,12,14,15,13,11,9},{16,18,20,22,23,21,19,17},{24..., dimensions={0} | all-to-all | bytes 1048576 | tf_op jit(solution)/shard_map/all_to_all | solution.py:363
  23.9 3.0 %collective-permute-start = (f32[8,2,16,512]{3,2,1,0:T(8,128)S(1)}, f32[8,2,16,512]{3,2,1,0:T(8,128)S(1)}, u32[]{:S(2)}, u32[]{:S(2)}) collective-permute-start(f32[8,2,16,512]{3,2,1,0:T(8,128)S(1)} %all_to_all.10.own_ref), channel_id=1, source_target_pairs={{0,8},{16,24},{8,0},{24,16},{1,9},{17,25},{9,1},{25,17},{2,10},{18... | collective-permute-start | bytes 1572872 | tf_op jit(solution)/shard_map/ppermute | solution.py:367
  26.8 3.0 %collective-permute-start.1 = (f32[8,2,16,512]{3,2,1,0:T(8,128)S(1)}, f32[8,2,16,512]{3,2,1,0:T(8,128)S(1)}, u32[]{:S(2)}, u32[]{:S(2)}) collective-permute-start(f32[8,2,16,512]{3,2,1,0:T(8,128)S(1)} %all_to_all.10.own_ref), channel_id=1, source_target_pairs={{8,16},{16,8},{9,17},{17,9},{10,18},{18,10},{11,19},{19,11},{12,20... | collective-permute-start | bytes 1572872 | tf_op jit(solution)/shard_map/ppermute | solution.py:367
  29.8 0.0 collective-permute-done.twin_ref
  29.8 0.0 copy-done.1
  29.9 0.0 copy-done.2
  29.9 0.0 copy-done
  29.9 0.0 copy-done.3
  29.9 0.0 copy-done.4
  29.9 0.0 copy-done.5
  29.9 4.1 %near.1 = (f32[8,2,16,512]{3,2,1,0:T(8,128)S(1)}, s32[8,25]{1,0:T(8,128)S(1)}, s32[8]{0:T(128)S(1)}, bf16[256,1536]{1,0:T(8,128)(2,1)S(1)}, bf16[256,256]{1,0:T(8,128)(2,1)S(1)}) custom-call(s32[8,24]{1,0:T(8,128)S(1)} %copy-done.3, s32[8,24]{1,0:T(8,128)S(1)} %copy-done.4, s32[8]{0:T(128)S(1)} %copy-done.5, s32[1]{0:T(128)} %bitcast.group_ref, ...), custom_call_target="tpu_custom_call" | custom-call | flops 50000000 | bytes 1048576 | tf_op jit(solution)/shard_map/near/pallas_call | solution.py:374
  34.0 3.3 %collective-permute-done.1.far_data_ref = f32[8,2,16,512]{3,2,1,0:T(8,128)S(1)} collective-permute-done((f32[8,2,16,512]{3,2,1,0:T(8,128)S(1)}, f32[8,2,16,512]{3,2,1,0:T(8,128)S(1)}, u32[]{:S(2)}, u32[]{:S(2)}) %collective-permute-start.1) | collective-permute-done | bytes 524320 | tf_op jit(solution)/shard_map/ppermute | solution.py:367
  37.3 1.4 %far.1 = f32[8,2,16,512]{3,2,1,0:T(8,128)S(1)} custom-call(s32[8,25]{1,0:T(8,128)S(1)} %get-tuple-element.14.far_ref, s32[8]{0:T(128)S(1)} %get-tuple-element.15.far_count_ref, f32[316,2,512]{2,1,0:T(2,128)S(1)} %bitcast.7, f32[8,2,16,512]{3,2,1,0:T(8,128)S(1)} %collective-permute-done.1.far_data_ref, f32[8,2,16,512]{3,2,1,0:T(8,128)S(1)} %get-tuple-element.16.near_ref), custom_call_target="tpu_custom_call" | custom-call | tf_op jit(solution)/shard_map/far/pallas_call | solution.py:394
  38.7 14.3 %all_to_all.11.r_ref = f32[8,2,16,512]{3,2,1,0:T(8,128)S(1)} all-to-all(f32[8,2,16,512]{3,2,1,0:T(8,128)S(1)} %far.1), channel_id=1, replica_groups={{0,2,4,6,7,5,3,1},{8,10,12,14,15,13,11,9},{16,18,20,22,23,21,19,17},{24..., dimensions={0} | all-to-all | bytes 1048576 | tf_op jit(solution)/shard_map/all_to_all | solution.py:363
  53.1 3.4 %disaggregate.1 = f32[2,32,4,8,128]{4,3,2,1,0:T(8,128)} custom-call(f32[8,2,16,512]{3,2,1,0:T(8,128)S(1)} %all_to_all.11.r_ref, bf16[256,1536]{1,0:T(8,128)(2,1)S(1)} %get-tuple-element.17.weights_ref, bf16[256,256]{1,0:T(8,128)(2,1)S(1)} %get-tuple-element.18.phi_weights_ref, f32[8,4096]{1,0:T(8,128)S(1)} %get-tuple-element.19.cos_ref, ...), custom_call_target="tpu_custom_call" | custom-call | tf_op jit(solution)/shard_map/disaggregate/pallas_call | solution.py:403
Async XLA Ops:
  0.0 29.8 %copy-start.1 = (f32[64,32]{0,1:T(8,128)S(1)}, f32[64,32]{0,1:T(8,128)}, u32[]{:S(2)}) copy-start(f32[64,32]{0,1:T(8,128)} %param.9) | copy-start | bytes 24580
  0.0 29.9 %copy-start.2 = (f32[64,32]{0,1:T(8,128)S(1)}, f32[64,32]{0,1:T(8,128)}, u32[]{:S(2)}) copy-start(f32[64,32]{0,1:T(8,128)} %param.10) | copy-start | bytes 24580
  0.0 29.9 %copy-start = (f32[2,316,512]{2,0,1:T(2,128)S(1)}, f32[2,316,512]{2,0,1:T(2,128)}, u32[]{:S(2)}) copy-start(f32[2,316,512]{2,0,1:T(2,128)} %param.12) | copy-start | bytes 3883012
  0.0 29.9 %copy-start.3 = (s32[8,24]{1,0:T(8,128)S(1)}, s32[8,24]{1,0:T(8,128)}, u32[]{:S(2)}) copy-start(s32[8,24]{1,0:T(8,128)} %source_ref.1) | copy-start | bytes 2308
  0.0 29.9 %copy-start.4 = (s32[8,24]{1,0:T(8,128)S(1)}, s32[8,24]{1,0:T(8,128)}, u32[]{:S(2)}) copy-start(s32[8,24]{1,0:T(8,128)} %kind_ref.1) | copy-start | bytes 2308
  0.0 29.9 %copy-start.5 = (s32[8]{0:T(128)S(1)}, s32[8]{0:T(128)}, u32[]{:S(2)}) copy-start(s32[8]{0:T(128)} %count_ref.1) | copy-start | bytes 100
  23.9 6.0 %collective-permute-start = (f32[8,2,16,512]{3,2,1,0:T(8,128)S(1)}, f32[8,2,16,512]{3,2,1,0:T(8,128)S(1)}, u32[]{:S(2)}, u32[]{:S(2)}) collective-permute-start(f32[8,2,16,512]{3,2,1,0:T(8,128)S(1)} %all_to_all.10.own_ref), channel_id=1, source_target_pairs={{0,8},{16,24},{8,0},{24,16},{1,9},{17,25},{9,1},{25,17},{2,10},{18... | collective-permute-start | bytes 1572872 | tf_op jit(solution)/shard_map/ppermute | solution.py:367
  26.8 10.5 %collective-permute-start.1 = (f32[8,2,16,512]{3,2,1,0:T(8,128)S(1)}, f32[8,2,16,512]{3,2,1,0:T(8,128)S(1)}, u32[]{:S(2)}, u32[]{:S(2)}) collective-permute-start(f32[8,2,16,512]{3,2,1,0:T(8,128)S(1)} %all_to_all.10.own_ref), channel_id=1, source_target_pairs={{8,16},{16,8},{9,17},{17,9},{10,18},{18,10},{11,19},{19,11},{12,20... | collective-permute-start | bytes 1572872 | tf_op jit(solution)/shard_map/ppermute | solution.py:367

commit v5 on v4

--- a/solution.py
+++ b/solution.py
@@ -9,7 +9,7 @@
 bf16 = jnp.bfloat16
 SUB = 8
 BLOCK = 256
-UNROLL = 4
+UNROLL = 8
 PAIR = 16
 COST = 50_000_000
 VMEM_LIMIT = 20 << 20

time: 56.7 us -> 56.6 us (level)
  no operation moved by 1% of the time
where the time goes in v5:
time: 56.6 us; the launch traced here: 56.3 us
  blocking collectives  32.4 us (57%)
  Pallas kernels  14.6 us (26%)
  starting transfers between devices  5.96 us (11%)
  waiting for transfers between devices  3.22 us (6%)
    all_to_all x2, blocking collectives, exchange(): lax.all_to_all(x, 'mem', split_axis=0, concat_axis=0, tiled=True, axis_in...  32.4 us
    ppermute x2, starting transfers between devices, swap(): return lax.ppermute(x, 'grp', pairs + [(j, i) for i, j in pairs])  5.96 us
    pallas_call x1, Pallas kernels, per_device(): call(aggregate_kernel, out_shape=(shape(block, f32), shape(phases, f32),...  5.33 us
    pallas_call x1, Pallas kernels, per_device(): call(near_kernel, out_shape=(shape(block, f32), shape((targets, slots + 1...  4.18 us
    pallas_call x1, Pallas kernels, per_device(): call(disaggregate_kernel, out_shape=shape(field.shape, f32), in_specs=[vm...  3.46 us
    ppermute x2, waiting for transfers between devices, swap(): return lax.ppermute(x, 'grp', pairs + [(j, i) for i, j in pairs])  3.22 us
    pallas_call x1, Pallas kernels, per_device(): call(far_kernel, out_shape=shape(block, f32), in_specs=[smem()] * 2 + [vm...  1.65 us
  transfers between devices with their start and end apart: 2, of which 1 were waited for; matrix products, arithmetic and copies ran while one was open for 0% of the time, Pallas kernels for 7%

profile of v5, /device:TPU:1, one launch (start us, length us, event | category | flops | bytes accessed | tf_op | source)
XLA Modules:
  0.0 56.3 jit_solution(7207693818257754423)
XLA Ops:
  0.0 0.0 copy-start.1
  0.0 0.0 copy-start.2
  0.0 0.0 copy-start
  0.0 0.0 copy-start.3
  0.0 0.0 copy-start.4
  0.0 0.0 copy-start.5
  0.0 5.3 %aggregate.1 = (f32[8,2,16,512]{3,2,1,0:T(8,128)S(1)}, f32[8,4096]{1,0:T(8,128)S(1)}, f32[8,4096]{1,0:T(8,128)S(1)}) custom-call(f32[2,32,4,8,128]{4,3,2,1,0:T(8,128)} %bitcast.12, f32[32,64]{1,0:T(8,128)} %bitcast.8, f32[32,64]{1,0:T(8,128)} %bitcast.10, f32[8,4096]{1,0:T(8,128)} %phase_ref.1), custom_call_target="tpu_custom_call" | custom-call | tf_op jit(solution)/shard_map/aggregate/pallas_call | solution.py:344
  5.4 18.5 %all_to_all.10.own_ref = f32[8,2,16,512]{3,2,1,0:T(8,128)S(1)} all-to-all(f32[8,2,16,512]{3,2,1,0:T(8,128)S(1)} %get-tuple-element.13), channel_id=1, replica_groups={{0,2,4,6,7,5,3,1},{8,10,12,14,15,13,11,9},{16,18,20,22,23,21,19,17},{24..., dimensions={0} | all-to-all | bytes 1048576 | tf_op jit(solution)/shard_map/all_to_all | solution.py:363
  23.9 3.0 %collective-permute-start = (f32[8,2,16,512]{3,2,1,0:T(8,128)S(1)}, f32[8,2,16,512]{3,2,1,0:T(8,128)S(1)}, u32[]{:S(2)}, u32[]{:S(2)}) collective-permute-start(f32[8,2,16,512]{3,2,1,0:T(8,128)S(1)} %all_to_all.10.own_ref), channel_id=1, source_target_pairs={{0,8},{16,24},{8,0},{24,16},{1,9},{17,25},{9,1},{25,17},{2,10},{18... | collective-permute-start | bytes 1572872 | tf_op jit(solution)/shard_map/ppermute | solution.py:367
  26.8 3.0 %collective-permute-start.1 = (f32[8,2,16,512]{3,2,1,0:T(8,128)S(1)}, f32[8,2,16,512]{3,2,1,0:T(8,128)S(1)}, u32[]{:S(2)}, u32[]{:S(2)}) collective-permute-start(f32[8,2,16,512]{3,2,1,0:T(8,128)S(1)} %all_to_all.10.own_ref), channel_id=1, source_target_pairs={{8,16},{16,8},{9,17},{17,9},{10,18},{18,10},{11,19},{19,11},{12,20... | collective-permute-start | bytes 1572872 | tf_op jit(solution)/shard_map/ppermute | solution.py:367
  29.8 0.0 collective-permute-done.twin_ref
  29.8 0.0 copy-done.1
  29.9 0.0 copy-done.2
  29.9 0.0 copy-done
  29.9 0.0 copy-done.3
  29.9 0.0 copy-done.4
  29.9 0.0 copy-done.5
  29.9 4.2 %near.1 = (f32[8,2,16,512]{3,2,1,0:T(8,128)S(1)}, s32[8,25]{1,0:T(8,128)S(1)}, s32[8]{0:T(128)S(1)}, bf16[256,1536]{1,0:T(8,128)(2,1)S(1)}, bf16[256,256]{1,0:T(8,128)(2,1)S(1)}) custom-call(s32[8,24]{1,0:T(8,128)S(1)} %copy-done.3, s32[8,24]{1,0:T(8,128)S(1)} %copy-done.4, s32[8]{0:T(128)S(1)} %copy-done.5, s32[1]{0:T(128)} %bitcast.group_ref, ...), custom_call_target="tpu_custom_call" | custom-call | flops 50000000 | bytes 1048576 | tf_op jit(solution)/shard_map/near/pallas_call | solution.py:374
  34.1 3.2 %collective-permute-done.1.far_data_ref = f32[8,2,16,512]{3,2,1,0:T(8,128)S(1)} collective-permute-done((f32[8,2,16,512]{3,2,1,0:T(8,128)S(1)}, f32[8,2,16,512]{3,2,1,0:T(8,128)S(1)}, u32[]{:S(2)}, u32[]{:S(2)}) %collective-permute-start.1) | collective-permute-done | bytes 524320 | tf_op jit(solution)/shard_map/ppermute | solution.py:367
  37.3 1.6 %far.1 = f32[8,2,16,512]{3,2,1,0:T(8,128)S(1)} custom-call(s32[8,25]{1,0:T(8,128)S(1)} %get-tuple-element.14.far_ref, s32[8]{0:T(128)S(1)} %get-tuple-element.15.far_count_ref, f32[316,2,512]{2,1,0:T(2,128)S(1)} %bitcast.7, f32[8,2,16,512]{3,2,1,0:T(8,128)S(1)} %collective-permute-done.1.far_data_ref, f32[8,2,16,512]{3,2,1,0:T(8,128)S(1)} %get-tuple-element.16.near_ref), custom_call_target="tpu_custom_call" | custom-call | tf_op jit(solution)/shard_map/far/pallas_call | solution.py:394
  39.0 13.9 %all_to_all.11.r_ref = f32[8,2,16,512]{3,2,1,0:T(8,128)S(1)} all-to-all(f32[8,2,16,512]{3,2,1,0:T(8,128)S(1)} %far.1), channel_id=1, replica_groups={{0,2,4,6,7,5,3,1},{8,10,12,14,15,13,11,9},{16,18,20,22,23,21,19,17},{24..., dimensions={0} | all-to-all | bytes 1048576 | tf_op jit(solution)/shard_map/all_to_all | solution.py:363
  52.9 3.5 %disaggregate.1 = f32[2,32,4,8,128]{4,3,2,1,0:T(8,128)} custom-call(f32[8,2,16,512]{3,2,1,0:T(8,128)S(1)} %all_to_all.11.r_ref, bf16[256,1536]{1,0:T(8,128)(2,1)S(1)} %get-tuple-element.17.weights_ref, bf16[256,256]{1,0:T(8,128)(2,1)S(1)} %get-tuple-element.18.phi_weights_ref, f32[8,4096]{1,0:T(8,128)S(1)} %get-tuple-element.19.cos_ref, ...), custom_call_target="tpu_custom_call" | custom-call | tf_op jit(solution)/shard_map/disaggregate/pallas_call | solution.py:403
Async XLA Ops:
  0.0 29.8 %copy-start.1 = (f32[64,32]{0,1:T(8,128)S(1)}, f32[64,32]{0,1:T(8,128)}, u32[]{:S(2)}) copy-start(f32[64,32]{0,1:T(8,128)} %param.9) | copy-start | bytes 24580
  0.0 29.9 %copy-start.2 = (f32[64,32]{0,1:T(8,128)S(1)}, f32[64,32]{0,1:T(8,128)}, u32[]{:S(2)}) copy-start(f32[64,32]{0,1:T(8,128)} %param.10) | copy-start | bytes 24580
  0.0 29.9 %copy-start = (f32[2,316,512]{2,0,1:T(2,128)S(1)}, f32[2,316,512]{2,0,1:T(2,128)}, u32[]{:S(2)}) copy-start(f32[2,316,512]{2,0,1:T(2,128)} %param.12) | copy-start | bytes 3883012
  0.0 29.9 %copy-start.3 = (s32[8,24]{1,0:T(8,128)S(1)}, s32[8,24]{1,0:T(8,128)}, u32[]{:S(2)}) copy-start(s32[8,24]{1,0:T(8,128)} %source_ref.1) | copy-start | bytes 2308
  0.0 29.9 %copy-start.4 = (s32[8,24]{1,0:T(8,128)S(1)}, s32[8,24]{1,0:T(8,128)}, u32[]{:S(2)}) copy-start(s32[8,24]{1,0:T(8,128)} %kind_ref.1) | copy-start | bytes 2308
  0.0 29.9 %copy-start.5 = (s32[8]{0:T(128)S(1)}, s32[8]{0:T(128)}, u32[]{:S(2)}) copy-start(s32[8]{0:T(128)} %count_ref.1) | copy-start | bytes 100
  23.9 6.0 %collective-permute-start = (f32[8,2,16,512]{3,2,1,0:T(8,128)S(1)}, f32[8,2,16,512]{3,2,1,0:T(8,128)S(1)}, u32[]{:S(2)}, u32[]{:S(2)}) collective-permute-start(f32[8,2,16,512]{3,2,1,0:T(8,128)S(1)} %all_to_all.10.own_ref), channel_id=1, source_target_pairs={{0,8},{16,24},{8,0},{24,16},{1,9},{17,25},{9,1},{25,17},{2,10},{18... | collective-permute-start | bytes 1572872 | tf_op jit(solution)/shard_map/ppermute | solution.py:367
  26.8 10.5 %collective-permute-start.1 = (f32[8,2,16,512]{3,2,1,0:T(8,128)S(1)}, f32[8,2,16,512]{3,2,1,0:T(8,128)S(1)}, u32[]{:S(2)}, u32[]{:S(2)}) collective-permute-start(f32[8,2,16,512]{3,2,1,0:T(8,128)S(1)} %all_to_all.10.own_ref), channel_id=1, source_target_pairs={{8,16},{16,8},{9,17},{17,9},{10,18},{18,10},{11,19},{19,11},{12,20... | collective-permute-start | bytes 1572872 | tf_op jit(solution)/shard_map/ppermute | solution.py:367

commit v6 on v5

--- a/solution.py
+++ b/solution.py
@@ -10,6 +10,7 @@
 SUB = 8
 BLOCK = 256
 UNROLL = 8
+FAR_UNROLL = 4
 PAIR = 16
 COST = 50_000_000
 VMEM_LIMIT = 20 << 20
@@ -140,11 +141,11 @@
     lax.fori_loop(0, fine // batch, body, 0)
 
 
-def add_slots(entry_of, count, factor_ref, data_ref, acc, wide):
+def add_slots(entry_of, count, factor_ref, data_ref, acc, wide, unroll):
     def slot_body(step, acc):
         real, imag = acc
-        for i in range(UNROLL):
-            k = step * UNROLL + i
+        for i in range(unroll):
+            k = step * unroll + i
             live = k < count
             entry = jnp.where(live, entry_of(k), 0)
             kind = lax.div(entry, wide)
@@ -158,7 +159,7 @@
             imag = imag + (fr * si + fi * sr)
         return real, imag
 
-    return lax.fori_loop(0, lax.div(count + (UNROLL - 1), UNROLL), slot_body, acc)
+    return lax.fori_loop(0, lax.div(count + (unroll - 1), unroll), slot_body, acc)
 
 
 def near_kernel(source_ref, kind_ref, count_ref, group_ref, factor_ref, own_ref, twin_ref, theta_ref, phi_ref, o_ref, far_ref, far_count_ref, theta_out, phi_out, list_ref, near_count_ref, all_ref):
@@ -196,7 +197,7 @@
 
     def target_body(t, carry):
         zero = jnp.zeros((waves, directions), f32)
-        real, imag = add_slots(lambda k: list_ref[t, k], near_count_ref[t], factor_ref, all_ref, (zero, zero), wide)
+        real, imag = add_slots(lambda k: list_ref[t, k], near_count_ref[t], factor_ref, all_ref, (zero, zero), wide, UNROLL)
         o_ref[t, 0] = real
         o_ref[t, 1] = imag
         return carry
@@ -232,7 +233,7 @@
 
     def target_body(t, carry):
         acc = near_ref[t, 0], near_ref[t, 1]
-        real, imag = add_slots(lambda k: far_ref[t, k], far_count_ref[t], factor_ref, data_ref, acc, wide)
+        real, imag = add_slots(lambda k: far_ref[t, k], far_count_ref[t], factor_ref, data_ref, acc, wide, FAR_UNROLL)
         o_ref[seat(t, targets), 0] = real
         o_ref[seat(t, targets), 1] = imag
         return carry

time: 56.6 us -> 56.6 us (level)
  no operation moved by 1% of the time
where the time goes in v6:
time: 56.6 us; the launch traced here: 56.4 us
  blocking collectives  32.7 us (58%)
  Pallas kernels  14.4 us (25%)
  starting transfers between devices  5.96 us (11%)
  waiting for transfers between devices  3.22 us (6%)
    all_to_all x2, blocking collectives, exchange(): lax.all_to_all(x, 'mem', split_axis=0, concat_axis=0, tiled=True, axis_in...  32.7 us
    ppermute x2, starting transfers between devices, swap(): return lax.ppermute(x, 'grp', pairs + [(j, i) for i, j in pairs])  5.96 us
    pallas_call x1, Pallas kernels, per_device(): call(aggregate_kernel, out_shape=(shape(block, f32), shape(phases, f32),...  5.33 us
    pallas_call x1, Pallas kernels, per_device(): call(near_kernel, out_shape=(shape(block, f32), shape((targets, slots + 1...  4.18 us
    pallas_call x1, Pallas kernels, per_device(): call(disaggregate_kernel, out_shape=shape(field.shape, f32), in_specs=[vm...  3.46 us
    ppermute x2, waiting for transfers between devices, swap(): return lax.ppermute(x, 'grp', pairs + [(j, i) for i, j in pairs])  3.22 us
    pallas_call x1, Pallas kernels, per_device(): call(far_kernel, out_shape=shape(block, f32), in_specs=[smem()] * 2 + [vm...  1.42 us
  transfers between devices with their start and end apart: 2, of which 1 were waited for; matrix products, arithmetic and copies ran while one was open for 0% of the time, Pallas kernels for 7%

profile of v6, /device:TPU:1, one launch (start us, length us, event | category | flops | bytes accessed | tf_op | source)
XLA Modules:
  0.0 56.4 jit_solution(7775070115726421063)
XLA Ops:
  0.0 0.0 copy-start.1
  0.0 0.0 copy-start.2
  0.0 0.0 copy-start
  0.0 0.0 copy-start.3
  0.0 0.0 copy-start.4
  0.0 0.0 copy-start.5
  0.0 5.3 %aggregate.1 = (f32[8,2,16,512]{3,2,1,0:T(8,128)S(1)}, f32[8,4096]{1,0:T(8,128)S(1)}, f32[8,4096]{1,0:T(8,128)S(1)}) custom-call(f32[2,32,4,8,128]{4,3,2,1,0:T(8,128)} %bitcast.12, f32[32,64]{1,0:T(8,128)} %bitcast.8, f32[32,64]{1,0:T(8,128)} %bitcast.10, f32[8,4096]{1,0:T(8,128)} %phase_ref.1), custom_call_target="tpu_custom_call" | custom-call | tf_op jit(solution)/shard_map/aggregate/pallas_call | solution.py:345
  5.4 18.5 %all_to_all.10.own_ref = f32[8,2,16,512]{3,2,1,0:T(8,128)S(1)} all-to-all(f32[8,2,16,512]{3,2,1,0:T(8,128)S(1)} %get-tuple-element.13), channel_id=1, replica_groups={{0,2,4,6,7,5,3,1},{8,10,12,14,15,13,11,9},{16,18,20,22,23,21,19,17},{24..., dimensions={0} | all-to-all | bytes 1048576 | tf_op jit(solution)/shard_map/all_to_all | solution.py:364
  23.9 3.0 %collective-permute-start = (f32[8,2,16,512]{3,2,1,0:T(8,128)S(1)}, f32[8,2,16,512]{3,2,1,0:T(8,128)S(1)}, u32[]{:S(2)}, u32[]{:S(2)}) collective-permute-start(f32[8,2,16,512]{3,2,1,0:T(8,128)S(1)} %all_to_all.10.own_ref), channel_id=1, source_target_pairs={{0,8},{16,24},{8,0},{24,16},{1,9},{17,25},{9,1},{25,17},{2,10},{18... | collective-permute-start | bytes 1572872 | tf_op jit(solution)/shard_map/ppermute | solution.py:368
  26.8 3.0 %collective-permute-start.1 = (f32[8,2,16,512]{3,2,1,0:T(8,128)S(1)}, f32[8,2,16,512]{3,2,1,0:T(8,128)S(1)}, u32[]{:S(2)}, u32[]{:S(2)}) collective-permute-start(f32[8,2,16,512]{3,2,1,0:T(8,128)S(1)} %all_to_all.10.own_ref), channel_id=1, source_target_pairs={{8,16},{16,8},{9,17},{17,9},{10,18},{18,10},{11,19},{19,11},{12,20... | collective-permute-start | bytes 1572872 | tf_op jit(solution)/shard_map/ppermute | solution.py:368
  29.8 0.0 collective-permute-done.twin_ref
  29.8 0.0 copy-done.1
  29.9 0.0 copy-done.2
  29.9 0.0 copy-done
  29.9 0.0 copy-done.3
  29.9 0.0 copy-done.4
  29.9 0.0 copy-done.5
  29.9 4.2 %near.1 = (f32[8,2,16,512]{3,2,1,0:T(8,128)S(1)}, s32[8,25]{1,0:T(8,128)S(1)}, s32[8]{0:T(128)S(1)}, bf16[256,1536]{1,0:T(8,128)(2,1)S(1)}, bf16[256,256]{1,0:T(8,128)(2,1)S(1)}) custom-call(s32[8,24]{1,0:T(8,128)S(1)} %copy-done.3, s32[8,24]{1,0:T(8,128)S(1)} %copy-done.4, s32[8]{0:T(128)S(1)} %copy-done.5, s32[1]{0:T(128)} %bitcast.group_ref, ...), custom_call_target="tpu_custom_call" | custom-call | flops 50000000 | bytes 1048576 | tf_op jit(solution)/shard_map/near/pallas_call | solution.py:375
  34.1 3.2 %collective-permute-done.1.far_data_ref = f32[8,2,16,512]{3,2,1,0:T(8,128)S(1)} collective-permute-done((f32[8,2,16,512]{3,2,1,0:T(8,128)S(1)}, f32[8,2,16,512]{3,2,1,0:T(8,128)S(1)}, u32[]{:S(2)}, u32[]{:S(2)}) %collective-permute-start.1) | collective-permute-done | bytes 524320 | tf_op jit(solution)/shard_map/ppermute | solution.py:368
  37.3 1.4 %far.1 = f32[8,2,16,512]{3,2,1,0:T(8,128)S(1)} custom-call(s32[8,25]{1,0:T(8,128)S(1)} %get-tuple-element.14.far_ref, s32[8]{0:T(128)S(1)} %get-tuple-element.15.far_count_ref, f32[316,2,512]{2,1,0:T(2,128)S(1)} %bitcast.7, f32[8,2,16,512]{3,2,1,0:T(8,128)S(1)} %collective-permute-done.1.far_data_ref, f32[8,2,16,512]{3,2,1,0:T(8,128)S(1)} %get-tuple-element.16.near_ref), custom_call_target="tpu_custom_call" | custom-call | tf_op jit(solution)/shard_map/far/pallas_call | solution.py:395
  38.7 14.2 %all_to_all.11.r_ref = f32[8,2,16,512]{3,2,1,0:T(8,128)S(1)} all-to-all(f32[8,2,16,512]{3,2,1,0:T(8,128)S(1)} %far.1), channel_id=1, replica_groups={{0,2,4,6,7,5,3,1},{8,10,12,14,15,13,11,9},{16,18,20,22,23,21,19,17},{24..., dimensions={0} | all-to-all | bytes 1048576 | tf_op jit(solution)/shard_map/all_to_all | solution.py:364
  52.9 3.5 %disaggregate.1 = f32[2,32,4,8,128]{4,3,2,1,0:T(8,128)} custom-call(f32[8,2,16,512]{3,2,1,0:T(8,128)S(1)} %all_to_all.11.r_ref, bf16[256,1536]{1,0:T(8,128)(2,1)S(1)} %get-tuple-element.17.weights_ref, bf16[256,256]{1,0:T(8,128)(2,1)S(1)} %get-tuple-element.18.phi_weights_ref, f32[8,4096]{1,0:T(8,128)S(1)} %get-tuple-element.19.cos_ref, ...), custom_call_target="tpu_custom_call" | custom-call | tf_op jit(solution)/shard_map/disaggregate/pallas_call | solution.py:404
Async XLA Ops:
  0.0 29.8 %copy-start.1 = (f32[64,32]{0,1:T(8,128)S(1)}, f32[64,32]{0,1:T(8,128)}, u32[]{:S(2)}) copy-start(f32[64,32]{0,1:T(8,128)} %param.9) | copy-start | bytes 24580
  0.0 29.9 %copy-start.2 = (f32[64,32]{0,1:T(8,128)S(1)}, f32[64,32]{0,1:T(8,128)}, u32[]{:S(2)}) copy-start(f32[64,32]{0,1:T(8,128)} %param.10) | copy-start | bytes 24580
  0.0 29.9 %copy-start = (f32[2,316,512]{2,0,1:T(2,128)S(1)}, f32[2,316,512]{2,0,1:T(2,128)}, u32[]{:S(2)}) copy-start(f32[2,316,512]{2,0,1:T(2,128)} %param.12) | copy-start | bytes 3883012
  0.0 29.9 %copy-start.3 = (s32[8,24]{1,0:T(8,128)S(1)}, s32[8,24]{1,0:T(8,128)}, u32[]{:S(2)}) copy-start(s32[8,24]{1,0:T(8,128)} %source_ref.1) | copy-start | bytes 2308
  0.0 29.9 %copy-start.4 = (s32[8,24]{1,0:T(8,128)S(1)}, s32[8,24]{1,0:T(8,128)}, u32[]{:S(2)}) copy-start(s32[8,24]{1,0:T(8,128)} %kind_ref.1) | copy-start | bytes 2308
  0.0 29.9 %copy-start.5 = (s32[8]{0:T(128)S(1)}, s32[8]{0:T(128)}, u32[]{:S(2)}) copy-start(s32[8]{0:T(128)} %count_ref.1) | copy-start | bytes 100
  23.9 6.0 %collective-permute-start = (f32[8,2,16,512]{3,2,1,0:T(8,128)S(1)}, f32[8,2,16,512]{3,2,1,0:T(8,128)S(1)}, u32[]{:S(2)}, u32[]{:S(2)}) collective-permute-start(f32[8,2,16,512]{3,2,1,0:T(8,128)S(1)} %all_to_all.10.own_ref), channel_id=1, source_target_pairs={{0,8},{16,24},{8,0},{24,16},{1,9},{17,25},{9,1},{25,17},{2,10},{18... | collective-permute-start | bytes 1572872 | tf_op jit(solution)/shard_map/ppermute | solution.py:368
  26.8 10.5 %collective-permute-start.1 = (f32[8,2,16,512]{3,2,1,0:T(8,128)S(1)}, f32[8,2,16,512]{3,2,1,0:T(8,128)S(1)}, u32[]{:S(2)}, u32[]{:S(2)}) collective-permute-start(f32[8,2,16,512]{3,2,1,0:T(8,128)S(1)} %all_to_all.10.own_ref), channel_id=1, source_target_pairs={{8,16},{16,8},{9,17},{17,9},{10,18},{18,10},{11,19},{19,11},{12,20... | collective-permute-start | bytes 1572872 | tf_op jit(solution)/shard_map/ppermute | solution.py:368
